TPU v7x, 32 devices: a whole 2x2x4 slice. The times are simulated.
32 devices in a mesh: groups: 2 (over y), ctx: 4 (over z), ep: 2 (over x), tp: 2 (over core).
Axes of the slice: x: 2, y: 2, z: 4, core: 2. Of those that a mesh axis runs over, the one named last changes fastest.
Arguments:
- queries: bfloat16 [4, 512, 5120], P(('groups', 'ep'), 'ctx', 'tp'), parts along dimension 0, may hold values from -128 to 128
- keys: bfloat16 [4, 512, 1024], P(('groups', 'ep'), 'ctx', 'tp'), parts along dimension 0, may hold values from -6 to 6
- values: bfloat16 [4, 512, 1024], P(('groups', 'ep'), 'ctx', 'tp'), parts along dimension 0, may hold values from -6 to 6
- expert_ids: int32 [4, 512, 1], P(('groups', 'ep'), 'ctx'), parts along dimension 0, may hold values from 0 to 127, as said below
- router: bfloat16 [5120, 2], P('tp', 'ep'), may hold values from -0.3125 to 0.3125
- w_gate: bfloat16 [2, 5120, 4096], P('ep', 'tp', 'ctx'), may hold values from -0.3125 to 0.3125
- w_up: bfloat16 [2, 5120, 4096], P('ep', 'tp', 'ctx'), may hold values from -0.3125 to 0.3125
- w_down: bfloat16 [2, 4096, 5120], P('ep', 'ctx', 'tp'), may hold values from -0.09375 to 0.09375
Outputs:
- layer_out: bfloat16 [4, 512, 5120], P(('groups', 'ep'), 'ctx', 'tp'), parts along dimension 0
There are 2 independent parts, one for each index of `groups`. A program takes and returns all parts, laid end to end along the dimension named above; an argument that names none is the same for every part. Nothing has to cross between parts.
Inputs may be any that keep to these rules, and one draw needn't show every extreme that they name: `expert_ids`: among the positions of one device, each expert below 2 is named at most 2 times; in every draw one of them is named exactly 2 times on every device.
All inputs are finite; a program needn't handle non-finite values.
Results may differ from a plain program's by a relative error of at most 0.023.
Values may be sent and summed in bfloat16 or wider, within the bound.
A program may use at most 64 MiB of HBM per device.

v0:
```python
import functools
import math

import jax
import jax.numpy as jnp
from jax import lax
from jax.experimental import pallas as pl
from jax.experimental.pallas import tpu as pltpu
from jax.sharding import PartitionSpec as P

HEAD_WIDTH = 128
CAP = 2
MESH = pl.DeviceIdType.MESH
MASKED = -1e30
EXP2_SCALE = HEAD_WIDTH ** (-0.5) * math.log2(math.e)


def tiles_of(width, tile):
    tile = min(width, tile)
    return [(start, min(tile, width - start)) for start in range(0, width, tile)]


def each(count, body):
    if count <= 8:
        for index in range(count):
            body(index)
    else:
        pl.loop(0, count)(body)


def kernel(
    n_ctx, n_ep, n_tp,
    ids_ref, router_ref, q_ref, k_ref, v_ref, wg_hbm, wu_hbm, wd_hbm,
    out_ref,
    wg, wu, wd, kbuf, vbuf, acc, row_max, totals, att,
    q_out, q_in, q_all, part_out, part_got, part_all, lse_out, lse_in, lse_all, out_rows, in_rows, members_f32, part, part_in, score, score_in, hidden,
    down_out, down_in, returned,
    w_sem, kv_send, kv_recv, row_send, row_recv, part_send, part_recv, score_sem,
    down_send, down_recv, q_send, q_recv, back_send, back_recv, lse_send, lse_recv,
):
    ctx = lax.axis_index("ctx")
    ep = lax.axis_index("ep")
    tp = lax.axis_index("tp")
    n = n_ctx * n_ep
    me = ep * n_ctx + ctx
    rows = q_ref.shape[1]
    features = q_ref.shape[2]
    kv_heads = k_ref.shape[2] // HEAD_WIDTH
    group = features // HEAD_WIDTH // kv_heads
    half = rows // 2
    fan = n_ctx // 2
    hidden_width = wg.shape[1]
    chunk_count, _, double_width = part.shape
    chunk_width = double_width // 2
    slots = returned.shape[0]
    places = features // HEAD_WIDTH

    w_copies = [
        pltpu.make_async_copy(src.at[0], dst, w_sem.at[index])
        for index, (src, dst) in enumerate(((wg_hbm, wg), (wu_hbm, wu), (wd_hbm, wd)))
    ]
    for copy in w_copies:
        copy.start()

    barrier = pltpu.get_barrier_semaphore()

    def greet(other):
        @pl.when(other != me)
        def _():
            pl.semaphore_signal(
                barrier, inc=1,
                device_id={"ep": other // n_ctx, "ctx": other % n_ctx},
                device_id_type=MESH,
            )

    each(n, greet)
    for step in range(1, n_tp):
        pl.semaphore_signal(
            barrier, inc=1, device_id={"tp": (tp + step) % n_tp}, device_id_type=MESH
        )
    ids = ids_ref[...]
    slot_row = lax.broadcasted_iota(jnp.int32, (slots, rows), 0)
    choose = jnp.where(ids == slot_row, 1.0, 0.0)
    below = lax.broadcasted_iota(jnp.int32, (rows, rows), 0)
    across = lax.broadcasted_iota(jnp.int32, (rows, rows), 1)
    strict = jnp.where(below < across, 1.0, 0.0).astype(jnp.bfloat16)
    earlier = jnp.dot(choose.astype(jnp.bfloat16), strict, preferred_element_type=jnp.float32)
    slot_index = jnp.sum(earlier * choose, axis=0, keepdims=True).astype(jnp.int32)
    target_row = jnp.where(ids < n_ep, ids * CAP + slot_index, -1)
    spread = jnp.where(target_row == slot_row, 1.0, 0.0).astype(jnp.bfloat16)
    live = n_ep * CAP
    lane_row = lax.broadcasted_iota(jnp.int32, (slots, rows), 1)
    row_place = jnp.sum(
        jnp.where(target_row == slot_row, lane_row, 0), axis=1, keepdims=True
    )
    q_all[...] = jnp.zeros_like(q_all)
    own_span = pl.ds(pl.multiple_of(ctx * slots, 8), slots)
    for start, size in tiles_of(features, 512):
        picked = jnp.dot(
            spread, q_ref[0, :, start:start + size], preferred_element_type=jnp.float32
        )
        q_all[own_span, start:start + size] = picked
        q_out[:, start:start + size] = picked[:live].astype(jnp.bfloat16)

    pl.semaphore_wait(barrier, n - 1 + n_tp - 1)

    def own_copy(piece):
        origin, buf = (k_ref, kbuf) if piece < 2 else (v_ref, vbuf)
        span = pl.ds((piece % 2) * half, half)
        return pltpu.make_async_remote_copy(
            src_ref=origin.at[0, span],
            dst_ref=buf.at[ctx, span],
            send_sem=kv_send.at[ctx, piece],
            recv_sem=kv_recv.at[ctx, piece],
            device_id={"ctx": ctx + 1},
            device_id_type=MESH,
        )

    def block_piece(block, piece):
        buf = kbuf if piece < 2 else vbuf
        span = pl.ds((piece % 2) * half, half)
        return pltpu.make_async_remote_copy(
            src_ref=buf.at[block, span],
            dst_ref=buf.at[block, span],
            send_sem=kv_send.at[block, piece],
            recv_sem=kv_recv.at[block, piece],
            device_id={"ctx": ctx + 1},
            device_id_type=MESH,
        )

    def push_own(first, last):
        @pl.when(ctx < n_ctx - 1)
        def _():
            for piece in range(first, last):
                own_copy(piece).start()

    def relay(block, first, last):
        @pl.when(block >= 0)
        def _():
            for piece in range(first, last):
                copy = block_piece(block, piece)
                copy.wait_recv()

                @pl.when(ctx < n_ctx - 1)
                def _():
                    copy.start()

    def q_copy(source, target):
        return pltpu.make_async_remote_copy(
            src_ref=q_out, dst_ref=q_in.at[source],
            send_sem=q_send.at[target], recv_sem=q_recv.at[source],
            device_id={"ctx": target}, device_id_type=MESH,
        )

    def back_copies(source, target):
        return [
            pltpu.make_async_remote_copy(
                src_ref=out.at[target], dst_ref=into.at[source],
                send_sem=sent.at[target], recv_sem=got.at[source],
                device_id={"ctx": target}, device_id_type=MESH,
            )
            for out, into, sent, got in (
                (part_out, part_got, back_send, back_recv),
                (lse_out, lse_in, lse_send, lse_recv),
            )
        ]

    def lower(body):
        def one(other):
            @pl.when(other < ctx)
            def _():
                body(other)

        each(n_ctx, one)

    def upper(body):
        def one(other):
            @pl.when(other > ctx)
            def _():
                body(other)

        each(n_ctx, one)

    lower(lambda other: q_copy(ctx, other).start())
    push_own(0, 2)

    kbuf[ctx] = k_ref[0]
    vbuf[ctx] = v_ref[0]
    acc[...] = jnp.zeros_like(acc)
    totals[...] = jnp.zeros_like(totals)
    row_max[...] = jnp.full_like(row_max, MASKED)

    query_offset = lax.broadcasted_iota(jnp.int32, (rows, rows), 0)
    key_offset = lax.broadcasted_iota(jnp.int32, (rows, rows), 1)
    offset_gap = query_offset - key_offset

    def process(block):
        visible = offset_gap >= (block - ctx) * rows
        visible = jnp.concatenate([visible] * group, axis=0)
        for head in range(kv_heads):
            lanes = slice(head * HEAD_WIDTH, (head + 1) * HEAD_WIDTH)
            stacked = jnp.concatenate(
                [
                    q_ref[0, :, (head * group + j) * HEAD_WIDTH:(head * group + j + 1) * HEAD_WIDTH]
                    for j in range(group)
                ],
                axis=0,
            )
            raw = lax.dot_general(
                stacked, kbuf[block, :, lanes], (((1,), (1,)), ((), ())),
                preferred_element_type=jnp.float32,
            )
            raw = jnp.where(visible, raw, MASKED)
            old_max = row_max[head]
            new_max = jnp.maximum(old_max, jnp.max(raw, axis=1, keepdims=True))
            factor = jnp.exp2((old_max - new_max) * EXP2_SCALE)
            weights = jnp.exp2((raw - new_max[:, :rows]) * EXP2_SCALE)
            row_max[head] = new_max
            totals[head] = totals[head] * factor + jnp.sum(weights, axis=1, keepdims=True)
            update = jnp.dot(
                weights.astype(jnp.bfloat16), vbuf[block, :, lanes],
                preferred_element_type=jnp.float32,
            )
            acc[head] = acc[head] * factor + update

    part_all[...] = jnp.zeros_like(part_all)
    lse_all[...] = jnp.full_like(lse_all, MASKED)
    source_row = lax.broadcasted_iota(jnp.int32, (n_ctx * slots, 1), 0) // slots
    limit = jnp.where(
        source_row == ctx, jnp.concatenate([row_place] * n_ctx, axis=0), rows
    )
    limit = jnp.concatenate([limit] * group, axis=0)
    upper(lambda other: q_copy(other, other).wait_recv())

    for other in range(n_ctx):
        @pl.when(other > ctx)
        def _():
            q_all[other * slots:other * slots + live, :] = q_in[other].astype(jnp.float32)

    tall = n_ctx * slots
    key_lane = lax.broadcasted_iota(jnp.int32, (group * tall, rows), 1)
    seen = key_lane <= limit
    head_lane = lax.broadcasted_iota(jnp.int32, (tall, 128), 1)
    lse = jnp.zeros((tall, 128), jnp.float32)
    for head in range(kv_heads):
        lanes = slice(head * HEAD_WIDTH, (head + 1) * HEAD_WIDTH)
        stacked = jnp.concatenate(
            [
                q_all[:, (head * group + j) * HEAD_WIDTH:(head * group + j + 1) * HEAD_WIDTH]
                for j in range(group)
            ],
            axis=0,
        ).astype(jnp.bfloat16)
        raw = lax.dot_general(
            stacked, k_ref[0, :, lanes], (((1,), (1,)), ((), ())),
            preferred_element_type=jnp.float32,
        )
        raw = jnp.where(seen, raw, MASKED)
        top = jnp.max(raw, axis=1, keepdims=True)
        weights = jnp.exp2((raw - top) * EXP2_SCALE)
        total = jnp.sum(weights, axis=1, keepdims=True)
        mixed = jnp.dot(
            weights.astype(jnp.bfloat16), v_ref[0, :, lanes],
            preferred_element_type=jnp.float32,
        ) / total
        column = top * EXP2_SCALE + jnp.log2(total)
        for j in range(group):
            place = head * group + j
            lse = jnp.where(head_lane == place, column[j * tall:(j + 1) * tall], lse)
            for other in range(n_ctx):
                first = j * tall + other * slots
                part_out[other, :, place * HEAD_WIDTH:(place + 1) * HEAD_WIDTH] = mixed[
                    first:first + live
                ].astype(jnp.bfloat16)
    for other in range(n_ctx):
        lse_out[other] = lse[other * slots:(other + 1) * slots]

    def give_back(other):
        for copy in back_copies(ctx, other):
            copy.start()

    upper(give_back)
    push_own(2, 4)

    def take_back(other):
        for copy in back_copies(other, other):
            copy.wait_recv()

    lower(take_back)
    for other in range(n_ctx):
        @pl.when(other < ctx)
        def _():
            part_all[other, :live] = part_got[other].astype(jnp.float32)
            lse_all[other] = lse_in[other]

        @pl.when(other == ctx)
        def _():
            part_all[other, :live] = part_out[other].astype(jnp.float32)
            lse_all[other] = lse_out[other]

    peak = jnp.max(lse_all[...], axis=0)
    shares = [jnp.exp2(lse_all[other] - peak) for other in range(n_ctx)]
    share_total = functools.reduce(jnp.add, shares)
    shares = [share / share_total for share in shares]
    for place in range(kv_heads * group):
        span = slice(place * HEAD_WIDTH, (place + 1) * HEAD_WIDTH)
        picked = shares[0][:, place:place + 1] * part_all[0, :, span]
        for other in range(1, n_ctx):
            picked = picked + shares[other][:, place:place + 1] * part_all[other, :, span]
        for expert in range(n_ep):
            out_rows[expert, place * CAP:(place + 1) * CAP] = picked[expert * CAP:(expert + 1) * CAP].astype(
                jnp.bfloat16
            )

    def row_copy(other, source):
        return pltpu.make_async_remote_copy(
            src_ref=out_rows.at[other // n_ctx],
            dst_ref=in_rows.at[source],
            send_sem=row_send.at[other],
            recv_sem=row_recv.at[source],
            device_id={"ep": other // n_ctx, "ctx": other % n_ctx},
            device_id_type=MESH,
        )

    def others(body):
        def one(step):
            @pl.when(step != me)
            def _():
                body(step)

        each(n, one)

    others(lambda other: row_copy(other, me).start())
    in_rows[me] = out_rows[ep]
    process(ctx)
    relay(ctx - 1, 0, 4)
    for copy in w_copies:
        copy.wait()
    others(lambda other: row_copy(other, other).wait_recv())

    def gather_member(index):
        dense = in_rows[index].astype(jnp.float32)
        for place in range(places):
            span = slice(place * HEAD_WIDTH, (place + 1) * HEAD_WIDTH)
            members_f32[index * CAP:(index + 1) * CAP, span] = dense[
                place * CAP:(place + 1) * CAP
            ]

    for index in range(n):
        gather_member(index)
    wide = members_f32[...]
    members = wide.astype(jnp.bfloat16)
    own_score = jnp.sum(wide * router_ref[...].astype(jnp.float32), axis=1, keepdims=True)
    score[...] = jnp.broadcast_to(own_score, score.shape).astype(jnp.bfloat16)
    peer = {"tp": n_tp - 1 - tp}
    score_copy = pltpu.make_async_remote_copy(
        src_ref=score, dst_ref=score_in, send_sem=score_sem.at[0], recv_sem=score_sem.at[1],
        device_id=peer, device_id_type=MESH,
    )
    score_copy.start()
    part_copies = []
    for chunk in range(chunk_count):
        span = slice(chunk * chunk_width, (chunk + 1) * chunk_width)
        part[chunk, :, :chunk_width] = jnp.dot(
            members, wg[:, span], preferred_element_type=jnp.float32
        ).astype(jnp.bfloat16)
        part[chunk, :, chunk_width:] = jnp.dot(
            members, wu[:, span], preferred_element_type=jnp.float32
        ).astype(jnp.bfloat16)
        copy = pltpu.make_async_remote_copy(
            src_ref=part.at[chunk], dst_ref=part_in.at[chunk],
            send_sem=part_send.at[chunk], recv_sem=part_recv.at[chunk],
            device_id=peer, device_id_type=MESH,
        )
        copy.start()
        part_copies.append(copy)
    relay(ctx - 2, 0, 2)
    score_copy.wait()
    gain = jax.nn.sigmoid(
        score[:, :1].astype(jnp.float32) + score_in[:, :1].astype(jnp.float32)
    )
    for chunk, copy in enumerate(part_copies):
        copy.wait()
        both = part[chunk].astype(jnp.float32) + part_in[chunk].astype(jnp.float32)
        gate = gain * both[:, :chunk_width]
        up = gain * both[:, chunk_width:]
        hidden[:, chunk * chunk_width:(chunk + 1) * chunk_width] = (
            gate * jax.nn.sigmoid(gate) * up
        ).astype(jnp.bfloat16)
    for start, size in tiles_of(features, 512):
        product = jnp.dot(
            hidden[...], wd[:, start:start + size], preferred_element_type=jnp.float32
        )
        for index in range(n):
            for place in range(start // HEAD_WIDTH, (start + size) // HEAD_WIDTH):
                lane = place * HEAD_WIDTH - start
                down_out[index, place * CAP:(place + 1) * CAP] = product[
                    index * CAP:(index + 1) * CAP, lane:lane + HEAD_WIDTH
                ].astype(jnp.bfloat16)

    def down_copy(other, source):
        return pltpu.make_async_remote_copy(
            src_ref=down_out.at[other],
            dst_ref=down_in.at[source],
            send_sem=down_send.at[other],
            recv_sem=down_recv.at[source],
            device_id={"ep": other // n_ctx, "ctx": other % n_ctx},
            device_id_type=MESH,
        )

    others(lambda other: down_copy(other, me).start())
    down_in[me] = down_out[me]
    returned[...] = jnp.zeros_like(returned)

    def visit(step, carry):
        block = ctx - step

        @pl.when(step == 2)
        def _():
            relay(block, 2, 4)

        @pl.when(step > 2)
        def _():
            relay(block, 0, 4)

        @pl.when(block >= 0)
        def _():
            process(block)

        return carry

    lax.fori_loop(1, n_ctx, visit, 0)

    for head in range(kv_heads):
        normed = (acc[head] / totals[head]).astype(jnp.bfloat16)
        for j in range(group):
            place = (head * group + j) * HEAD_WIDTH
            att[:, place:place + HEAD_WIDTH] = normed[j * rows:(j + 1) * rows]

    others(lambda other: row_copy(other, me).wait_send())
    lower(lambda other: q_copy(ctx, other).wait_send())

    def sent_back(other):
        for copy in back_copies(ctx, other):
            copy.wait_send()

    upper(sent_back)

    def drain(step, carry):
        block = ctx - step

        @pl.when((ctx < n_ctx - 1) & (block >= 0))
        def _():
            for piece in range(4):
                block_piece(block, piece).wait_send()

        return carry

    lax.fori_loop(0, n_ctx, drain, 0)

    others(lambda other: down_copy(other, other).wait_recv())
    for expert in range(n_ep):
        total = down_in[expert * n_ctx].astype(jnp.float32)
        for index in range(1, n_ctx):
            total = total + down_in[expert * n_ctx + index].astype(jnp.float32)
        total = total.astype(jnp.bfloat16).astype(jnp.float32)
        for place in range(places):
            span = slice(place * HEAD_WIDTH, (place + 1) * HEAD_WIDTH)
            returned[expert * CAP:(expert + 1) * CAP, span] = total[
                place * CAP:(place + 1) * CAP
            ]
    for start, size in tiles_of(features, 512):
        routed = lax.dot_general(
            spread, returned[:, start:start + size].astype(jnp.bfloat16),
            (((0,), (0,)), ((), ())), preferred_element_type=jnp.float32,
        )
        out_ref[0, :, start:start + size] = (
            att[:, start:start + size].astype(jnp.float32) + routed
        ).astype(jnp.bfloat16)
    others(lambda other: down_copy(other, me).wait_send())


def shards(queries, keys, values, expert_ids, router, w_gate, w_up, w_down):
    n_ctx, n_ep, n_tp = (lax.axis_size(axis) for axis in ("ctx", "ep", "tp"))
    n = n_ctx * n_ep
    _, rows, features = queries.shape
    kv_width = keys.shape[2]
    kv_heads = kv_width // HEAD_WIDTH
    group = features // kv_width
    hidden_width = w_gate.shape[2]
    chunk_width = min(hidden_width, 256)
    chunk_count = hidden_width // chunk_width
    members = n * CAP
    dense = features // HEAD_WIDTH * CAP
    live = n_ep * CAP
    slots = -(-live // 8) * 8
    bf16, f32 = jnp.bfloat16, jnp.float32
    vmem = pl.BlockSpec(memory_space=pltpu.VMEM)
    hbm = pl.BlockSpec(memory_space=pl.ANY)
    dma = pltpu.SemaphoreType.DMA
    return pl.pallas_call(
        functools.partial(kernel, n_ctx, n_ep, n_tp),
        out_shape=jax.ShapeDtypeStruct(queries.shape, bf16),
        in_specs=[vmem] * 5 + [hbm] * 3,
        out_specs=vmem,
        scratch_shapes=[
            pltpu.VMEM(w_gate.shape[1:], bf16),
            pltpu.VMEM(w_up.shape[1:], bf16),
            pltpu.VMEM(w_down.shape[1:], bf16),
            pltpu.VMEM((n_ctx, rows, kv_width), bf16),
            pltpu.VMEM((n_ctx, rows, kv_width), bf16),
            pltpu.VMEM((kv_heads, group * rows, HEAD_WIDTH), f32),
            pltpu.VMEM((kv_heads, group * rows, HEAD_WIDTH), f32),
            pltpu.VMEM((kv_heads, group * rows, HEAD_WIDTH), f32),
            pltpu.VMEM((rows, features), bf16),
            pltpu.VMEM((live, features), bf16),
            pltpu.VMEM((n_ctx, live, features), bf16),
            pltpu.VMEM((n_ctx * slots, features), f32),
            pltpu.VMEM((n_ctx, live, features), bf16),
            pltpu.VMEM((n_ctx, live, features), bf16),
            pltpu.VMEM((n_ctx, slots, features), f32),
            pltpu.VMEM((n_ctx, slots, 128), f32),
            pltpu.VMEM((n_ctx, slots, 128), f32),
            pltpu.VMEM((n_ctx, slots, 128), f32),
            pltpu.VMEM((n_ep, dense, HEAD_WIDTH), bf16),
            pltpu.VMEM((n, dense, HEAD_WIDTH), bf16),
            pltpu.VMEM((members, features), f32),
            pltpu.VMEM((chunk_count, members, 2 * chunk_width), bf16),
            pltpu.VMEM((chunk_count, members, 2 * chunk_width), bf16),
            pltpu.VMEM((members, 128), bf16),
            pltpu.VMEM((members, 128), bf16),
            pltpu.VMEM((members, hidden_width), bf16),
            pltpu.VMEM((n, dense, HEAD_WIDTH), bf16),
            pltpu.VMEM((n, dense, HEAD_WIDTH), bf16),
            pltpu.VMEM((slots, features), f32),
            dma((3,)),
            dma((n_ctx, 4)),
            dma((n_ctx, 4)),
            dma((n,)),
            dma((n,)),
            dma((chunk_count,)),
            dma((chunk_count,)),
            dma((2,)),
            dma((n,)),
            dma((n,)),
            dma((n_ctx,)),
            dma((n_ctx,)),
            dma((n_ctx,)),
            dma((n_ctx,)),
            dma((n_ctx,)),
            dma((n_ctx,)),
        ],
        compiler_params=pltpu.CompilerParams(
            collective_id=0, has_side_effects=True, vmem_limit_bytes=60 * 1024 * 1024
        ),
    )(
        expert_ids.reshape(1, rows), router.reshape(1, features), queries, keys, values,
        w_gate, w_up, w_down,
    )


def solution(mesh):
    placed = (
        P(("groups", "ep"), "ctx", "tp"),
        P(("groups", "ep"), "ctx", "tp"),
        P(("groups", "ep"), "ctx", "tp"),
        P(("groups", "ep"), "ctx", None),
        P("tp", "ep"),
        P("ep", "tp", "ctx"),
        P("ep", "tp", "ctx"),
        P("ep", "ctx", "tp"),
    )
    return jax.shard_map(
        shards,
        mesh=mesh,
        in_specs=placed,
        out_specs=P(("groups", "ep"), "ctx", "tp"),
        check_vma=False,
    )
```

profile of v0, /device:TPU:24, one launch (start us, length us, event | category | flops | bytes accessed | tf_op | source)
XLA Modules:
  0.0 32.1 jit_solution(15914343871489998575)
XLA Ops:
  0.0 30.1 %shard_map.82 = bf16[1,128,2560]{2,1,0:T(8,128)(2,1)} custom-call(s32[1,128]{1,0:T(1,128)} %bitcast.3, bf16[1,2560]{1,0:T(2,128)(2,1)} %bitcast.2, bf16[1,128,2560]{2,1,0:T(8,128)(2,1)} %q_ref.1, bf16[1,128,512]{2,1,0:T(8,128)(2,1)} %k_ref.1, bf16[1,128,512]{2,1,0:T(8,128)(2,1)} %v_ref.1, bf16[1,2560,1024]{2,1,0:T(8,128)(2,1)} %wg_hbm.1, ...), custom_call_target="tpu_custom_call" | custom-call | tf_op jit(solution)/shard_map/pallas_call | solution.py:501
  30.1 2.0 %copy.10 = bf16[1,128,2560]{2,1,0:T(8,128)(2,1)} copy(bf16[1,128,2560]{2,1,0:T(8,128)(2,1)} %shard_map.82) | data formatting | bytes 1310720
where the time goes:
time: 32.7 us; the launch traced here: 32.1 us
  Pallas kernels  30.1 us (92%)
  local copies, waits for them, and re-layouts  1.97 us (6%)
    pallas_call x1, Pallas kernels, shards(): pl.pallas_call(functools.partial(kernel, n_ctx, n_ep, n_tp), out_shape=ja...  30.1 us
    unnamed x1, local copies, waits for them, and re-layouts  1.97 us

commit v1 on v0

--- a/solution.py
+++ b/solution.py
@@ -30,12 +30,12 @@
 
 def kernel(
     n_ctx, n_ep, n_tp,
-    ids_ref, router_ref, q_ref, k_ref, v_ref, wg_hbm, wu_hbm, wd_hbm,
+    ids_hbm, router_hbm, q_hbm, k_hbm, v_hbm, wg_hbm, wu_hbm, wd_hbm,
     out_ref,
-    wg, wu, wd, kbuf, vbuf, acc, row_max, totals, att,
+    ids_ref, router_ref, q_ref, wg, wu, wd, kbuf, vbuf, acc, row_max, totals, att,
     q_out, q_in, q_all, part_out, part_got, part_all, lse_out, lse_in, lse_all, out_rows, in_rows, members_f32, part, part_in, score, score_in, hidden,
     down_out, down_in, returned,
-    w_sem, kv_send, kv_recv, row_send, row_recv, part_send, part_recv, score_sem,
+    w_sem, in_sem, kv_send, kv_recv, row_send, row_recv, part_send, part_recv, score_sem,
     down_send, down_recv, q_send, q_recv, back_send, back_recv, lse_send, lse_recv,
 ):
     ctx = lax.axis_index("ctx")
@@ -43,9 +43,8 @@
     tp = lax.axis_index("tp")
     n = n_ctx * n_ep
     me = ep * n_ctx + ctx
-    rows = q_ref.shape[1]
-    features = q_ref.shape[2]
-    kv_heads = k_ref.shape[2] // HEAD_WIDTH
+    rows, features = q_ref.shape
+    kv_heads = kbuf.shape[2] // HEAD_WIDTH
     group = features // HEAD_WIDTH // kv_heads
     half = rows // 2
     fan = n_ctx // 2
@@ -55,6 +54,15 @@
     slots = returned.shape[0]
     places = features // HEAD_WIDTH
 
+    in_copies = [
+        pltpu.make_async_copy(src, dst, in_sem.at[index])
+        for index, (src, dst) in enumerate((
+            (ids_hbm, ids_ref), (q_hbm.at[0], q_ref), (k_hbm.at[0], kbuf.at[ctx]),
+            (v_hbm.at[0], vbuf.at[ctx]), (router_hbm, router_ref),
+        ))
+    ]
+    for copy in in_copies:
+        copy.start()
     w_copies = [
         pltpu.make_async_copy(src.at[0], dst, w_sem.at[index])
         for index, (src, dst) in enumerate(((wg_hbm, wg), (wu_hbm, wu), (wd_hbm, wd)))
@@ -78,6 +86,7 @@
         pl.semaphore_signal(
             barrier, inc=1, device_id={"tp": (tp + step) % n_tp}, device_id_type=MESH
         )
+    in_copies[0].wait()
     ids = ids_ref[...]
     slot_row = lax.broadcasted_iota(jnp.int32, (slots, rows), 0)
     choose = jnp.where(ids == slot_row, 1.0, 0.0)
@@ -94,10 +103,11 @@
         jnp.where(target_row == slot_row, lane_row, 0), axis=1, keepdims=True
     )
     q_all[...] = jnp.zeros_like(q_all)
+    in_copies[1].wait()
     own_span = pl.ds(pl.multiple_of(ctx * slots, 8), slots)
     for start, size in tiles_of(features, 512):
         picked = jnp.dot(
-            spread, q_ref[0, :, start:start + size], preferred_element_type=jnp.float32
+            spread, q_ref[:, start:start + size], preferred_element_type=jnp.float32
         )
         q_all[own_span, start:start + size] = picked
         q_out[:, start:start + size] = picked[:live].astype(jnp.bfloat16)
@@ -105,16 +115,7 @@
     pl.semaphore_wait(barrier, n - 1 + n_tp - 1)
 
     def own_copy(piece):
-        origin, buf = (k_ref, kbuf) if piece < 2 else (v_ref, vbuf)
-        span = pl.ds((piece % 2) * half, half)
-        return pltpu.make_async_remote_copy(
-            src_ref=origin.at[0, span],
-            dst_ref=buf.at[ctx, span],
-            send_sem=kv_send.at[ctx, piece],
-            recv_sem=kv_recv.at[ctx, piece],
-            device_id={"ctx": ctx + 1},
-            device_id_type=MESH,
-        )
+        return block_piece(ctx, piece)
 
     def block_piece(block, piece):
         buf = kbuf if piece < 2 else vbuf
@@ -182,10 +183,10 @@
         each(n_ctx, one)
 
     lower(lambda other: q_copy(ctx, other).start())
+    in_copies[2].wait()
+    in_copies[3].wait()
     push_own(0, 2)
 
-    kbuf[ctx] = k_ref[0]
-    vbuf[ctx] = v_ref[0]
     acc[...] = jnp.zeros_like(acc)
     totals[...] = jnp.zeros_like(totals)
     row_max[...] = jnp.full_like(row_max, MASKED)
@@ -201,7 +202,7 @@
             lanes = slice(head * HEAD_WIDTH, (head + 1) * HEAD_WIDTH)
             stacked = jnp.concatenate(
                 [
-                    q_ref[0, :, (head * group + j) * HEAD_WIDTH:(head * group + j + 1) * HEAD_WIDTH]
+                    q_ref[:, (head * group + j) * HEAD_WIDTH:(head * group + j + 1) * HEAD_WIDTH]
                     for j in range(group)
                 ],
                 axis=0,
@@ -252,7 +253,7 @@
             axis=0,
         ).astype(jnp.bfloat16)
         raw = lax.dot_general(
-            stacked, k_ref[0, :, lanes], (((1,), (1,)), ((), ())),
+            stacked, kbuf[ctx, :, lanes], (((1,), (1,)), ((), ())),
             preferred_element_type=jnp.float32,
         )
         raw = jnp.where(seen, raw, MASKED)
@@ -260,7 +261,7 @@
         weights = jnp.exp2((raw - top) * EXP2_SCALE)
         total = jnp.sum(weights, axis=1, keepdims=True)
         mixed = jnp.dot(
-            weights.astype(jnp.bfloat16), v_ref[0, :, lanes],
+            weights.astype(jnp.bfloat16), vbuf[ctx, :, lanes],
             preferred_element_type=jnp.float32,
         ) / total
         column = top * EXP2_SCALE + jnp.log2(total)
@@ -348,6 +349,7 @@
 
     for index in range(n):
         gather_member(index)
+    in_copies[4].wait()
     wide = members_f32[...]
     members = wide.astype(jnp.bfloat16)
     own_score = jnp.sum(wide * router_ref[...].astype(jnp.float32), axis=1, keepdims=True)
@@ -496,14 +498,17 @@
     slots = -(-live // 8) * 8
     bf16, f32 = jnp.bfloat16, jnp.float32
     vmem = pl.BlockSpec(memory_space=pltpu.VMEM)
-    hbm = pl.BlockSpec(memory_space=pl.ANY)
+    hbm = pl.BlockSpec(memory_space=pltpu.HBM)
     dma = pltpu.SemaphoreType.DMA
     return pl.pallas_call(
         functools.partial(kernel, n_ctx, n_ep, n_tp),
-        out_shape=jax.ShapeDtypeStruct(queries.shape, bf16),
-        in_specs=[vmem] * 5 + [hbm] * 3,
+        out_shape=pltpu.VMEM(queries.shape, bf16),
+        in_specs=[hbm] * 8,
         out_specs=vmem,
         scratch_shapes=[
+            pltpu.VMEM((1, rows), jnp.int32),
+            pltpu.VMEM((1, features), bf16),
+            pltpu.VMEM((rows, features), bf16),
             pltpu.VMEM(w_gate.shape[1:], bf16),
             pltpu.VMEM(w_up.shape[1:], bf16),
             pltpu.VMEM(w_down.shape[1:], bf16),
@@ -534,6 +539,7 @@
             pltpu.VMEM((n, dense, HEAD_WIDTH), bf16),
             pltpu.VMEM((slots, features), f32),
             dma((3,)),
+            dma((5,)),
             dma((n_ctx, 4)),
             dma((n_ctx, 4)),
             dma((n,)),

time: 32.7 us -> 29.7 us (0.908); the launches traced: 32.1 us -> 29.5 us
  Pallas kernels: 30.1 us -> 28.6 us
  local copies, waits for them, and re-layouts: 1.97 us -> 0.84 us
    pallas_call x1, Pallas kernels: 30.1 us -> 28.6 us  [shards(): pl.pallas_call(functools.partial(kernel, n_ctx, n_ep, n_tp), out_shape=pl...]
    unnamed x1, local copies, waits for them, and re-layouts: 1.97 us -> 0.84 us
where the time goes in v1:
time: 29.7 us; the launch traced here: 29.5 us
  Pallas kernels  28.6 us (96%)
  local copies, waits for them, and re-layouts  0.84 us (3%)
    pallas_call x1, Pallas kernels, shards(): pl.pallas_call(functools.partial(kernel, n_ctx, n_ep, n_tp), out_shape=pl...  28.6 us
    unnamed x1, local copies, waits for them, and re-layouts  0.84 us

profile of v1, /device:TPU:24, one launch (start us, length us, event | category | flops | bytes accessed | tf_op | source)
XLA Modules:
  0.0 29.5 jit_solution(9311269977810096743)
XLA Ops:
  0.0 28.6 %shard_map.82 = bf16[1,128,2560]{2,1,0:T(8,128)(2,1)S(1)} custom-call(s32[1,128]{1,0:T(1,128)} %bitcast.3, bf16[1,2560]{1,0:T(2,128)(2,1)} %bitcast.2, bf16[1,128,2560]{2,1,0:T(8,128)(2,1)} %q_hbm.1, bf16[1,128,512]{2,1,0:T(8,128)(2,1)} %k_hbm.1, bf16[1,128,512]{2,1,0:T(8,128)(2,1)} %v_hbm.1, bf16[1,2560,1024]{2,1,0:T(8,128)(2,1)} %wg_hbm.1, ...), custom_call_target="tpu_custom_call" | custom-call | tf_op jit(solution)/shard_map/pallas_call | solution.py:503
  28.6 0.8 %copy.10 = bf16[1,128,2560]{2,1,0:T(8,128)(2,1)} copy(bf16[1,128,2560]{2,1,0:T(8,128)(2,1)S(1)} %shard_map.82) | data formatting | bytes 1310720

commit v2 on v1

v2 whole, which is shorter than its diff:
```python
import functools
import math

import jax
import jax.numpy as jnp
from jax import lax
from jax.experimental import pallas as pl
from jax.experimental.pallas import tpu as pltpu
from jax.sharding import PartitionSpec as P

HEAD_WIDTH = 128
CAP = 2
MESH = pl.DeviceIdType.MESH
MASKED = -1e30
EXP2_SCALE = HEAD_WIDTH ** (-0.5) * math.log2(math.e)
scope = jax.named_scope


def tiles_of(width, tile):
    tile = min(width, tile)
    return [(start, min(tile, width - start)) for start in range(0, width, tile)]


def padded(count, tile=8):
    return -(-count // tile) * tile


def each(count, body):
    if count <= 8:
        for index in range(count):
            body(index)
    else:
        pl.loop(0, count)(body)


def kernel(
    n_ctx, n_ep, n_tp,
    ids_hbm, router_hbm, q_hbm, k_hbm, v_hbm, wg_hbm, wu_hbm, wd_hbm,
    out_ref,
    ids_ref, router_ref, q_ref, wg, wu, wd, kv, acc, row_max, totals, att,
    q_own, q_out, q_in, q_all, part_out, part_got, part_all, lse_out, lse_in, lse_all,
    out_rows, in_rows,
    members_a, part_a, part_in_a, score_a, score_in_a, hidden_a,
    members_b, part_b, part_in_b, score_b, score_in_b, hidden_b,
    down_out, down_in, returned,
    in_sem, own_sem, w_sem, kv_send, kv_recv, row_send, row_recv,
    a_send, a_recv, a_score, b_send, b_recv, b_score,
    down_send, down_recv, q_send, q_recv, back_send, back_recv, lse_send, lse_recv,
):
    ctx = lax.axis_index("ctx")
    ep = lax.axis_index("ep")
    tp = lax.axis_index("tp")
    n = n_ctx * n_ep
    me = ep * n_ctx + ctx
    last = n_ctx - 1
    rows, features = q_ref.shape
    kv_heads = kv.shape[1]
    places = features // HEAD_WIDTH
    group = places // kv_heads
    slots = returned.shape[0]
    live = n_ep * CAP

    def lanes(place):
        return slice(place * HEAD_WIDTH, (place + 1) * HEAD_WIDTH)

    in_copies = [
        pltpu.make_async_copy(src, dst, in_sem.at[index])
        for index, (src, dst) in enumerate((
            (ids_hbm, ids_ref), (q_hbm.at[0], q_ref), (router_hbm, router_ref),
        ))
    ]
    own_copies = [
        pltpu.make_async_copy(
            src.at[0, :, lanes(head)], kv.at[ctx, head, which], own_sem.at[head, which]
        )
        for head in range(kv_heads)
        for which, src in enumerate((k_hbm, v_hbm))
    ]
    w_copies = [
        pltpu.make_async_copy(src.at[0], dst, w_sem.at[index])
        for index, (src, dst) in enumerate(((wg_hbm, wg), (wu_hbm, wu), (wd_hbm, wd)))
    ]
    for copy in in_copies[:2] + own_copies + in_copies[2:] + w_copies:
        copy.start()

    barrier = pltpu.get_barrier_semaphore()

    def greet(other):
        @pl.when(other != me)
        def _():
            pl.semaphore_signal(
                barrier, inc=1,
                device_id={"ep": other // n_ctx, "ctx": other % n_ctx},
                device_id_type=MESH,
            )

    each(n, greet)
    for step in range(1, n_tp):
        pl.semaphore_signal(
            barrier, inc=1, device_id={"tp": (tp + step) % n_tp}, device_id_type=MESH
        )

    def kv_copy(block, head):
        return pltpu.make_async_remote_copy(
            src_ref=kv.at[block, head], dst_ref=kv.at[block, head],
            send_sem=kv_send.at[block, head], recv_sem=kv_recv.at[block, head],
            device_id={"ctx": ctx + 1}, device_id_type=MESH,
        )

    def push_own(heads):
        @pl.when(ctx < last)
        def _():
            for head in heads:
                kv_copy(ctx, head).start()

    def relay(block, heads):
        @pl.when(block >= 0)
        def _():
            for head in heads:
                copy = kv_copy(block, head)
                copy.wait_recv()

                @pl.when(ctx < last)
                def _():
                    copy.start()

    def q_copy(source, target):
        return pltpu.make_async_remote_copy(
            src_ref=q_out, dst_ref=q_in.at[source],
            send_sem=q_send.at[target], recv_sem=q_recv.at[source],
            device_id={"ctx": target}, device_id_type=MESH,
        )

    def back_copies(source, target):
        return [
            pltpu.make_async_remote_copy(
                src_ref=out.at[target], dst_ref=into.at[source],
                send_sem=sent.at[target], recv_sem=got.at[source],
                device_id={"ctx": target}, device_id_type=MESH,
            )
            for out, into, sent, got in (
                (part_out, part_got, back_send, back_recv),
                (lse_out, lse_in, lse_send, lse_recv),
            )
        ]

    def to_index(other, out, into, sent, got, source):
        return pltpu.make_async_remote_copy(
            src_ref=out, dst_ref=into.at[source],
            send_sem=sent.at[other], recv_sem=got.at[source],
            device_id={"ep": other // n_ctx, "ctx": other % n_ctx}, device_id_type=MESH,
        )

    def row_copy(other, source):
        return to_index(other, out_rows.at[other // n_ctx], in_rows, row_send, row_recv, source)

    def down_copy(other, source):
        return to_index(other, down_out.at[other], down_in, down_send, down_recv, source)

    def lower(body):
        def one(other):
            @pl.when(other < ctx)
            def _():
                body(other)

        each(n_ctx, one)

    def upper(body):
        def one(step):
            other = last - step

            @pl.when(other > ctx)
            def _():
                body(other)

        each(n_ctx, one)

    def others(body):
        def one(other):
            @pl.when(other != me)
            def _():
                body(other)

        each(n, one)

    def first_owners(body):
        def one(expert):
            @pl.when(expert * n_ctx != me)
            def _():
                body(expert * n_ctx)

        each(n_ep, one)

    def later_owners(body):
        def one(other):
            @pl.when((other % n_ctx != 0) & (other != me))
            def _():
                body(other)

        each(n, one)

    with scope("a_pick"):
        in_copies[0].wait()
        ids = ids_ref[...]
        slot_row = lax.broadcasted_iota(jnp.int32, (slots, rows), 0)
        choose = jnp.where(ids == slot_row, 1.0, 0.0)
        below = lax.broadcasted_iota(jnp.int32, (rows, rows), 0)
        across = lax.broadcasted_iota(jnp.int32, (rows, rows), 1)
        strict = jnp.where(below < across, 1.0, 0.0).astype(jnp.bfloat16)
        earlier = jnp.dot(
            choose.astype(jnp.bfloat16), strict, preferred_element_type=jnp.float32
        )
        slot_index = jnp.sum(earlier * choose, axis=0, keepdims=True).astype(jnp.int32)
        target_row = jnp.where(ids < n_ep, ids * CAP + slot_index, -1)
        spread = jnp.where(target_row == slot_row, 1.0, 0.0).astype(jnp.bfloat16)
        lane_row = lax.broadcasted_iota(jnp.int32, (slots, rows), 1)
        row_place = jnp.sum(
            jnp.where(target_row == slot_row, lane_row, 0), axis=1, keepdims=True
        )
        in_copies[1].wait()
        for start, size in tiles_of(features, 512):
            picked = jnp.dot(
                spread, q_ref[:, start:start + size], preferred_element_type=jnp.float32
            )
            q_own[:, start:start + size] = picked
            q_out[:, start:start + size] = picked[:live].astype(jnp.bfloat16)

    def attend(source, tall, seen):
        raws = []
        for head in range(kv_heads):
            stacked = jnp.concatenate(
                [source[:, lanes(head * group + j)] for j in range(group)], axis=0
            ).astype(jnp.bfloat16)
            raw = lax.dot_general(
                stacked, kv[ctx, head, 0], (((1,), (1,)), ((), ())),
                preferred_element_type=jnp.float32,
            )
            raws.append(raw if seen is None else jnp.where(seen, raw, MASKED))
        tops = [jnp.max(raw, axis=1, keepdims=True) for raw in raws]
        weights = [jnp.exp2((raw - top) * EXP2_SCALE) for raw, top in zip(raws, tops)]
        sums = [jnp.sum(weight, axis=1, keepdims=True) for weight in weights]
        mixed = [
            jnp.dot(
                weight.astype(jnp.bfloat16), kv[ctx, head, 1],
                preferred_element_type=jnp.float32,
            ) / total
            for head, (weight, total) in enumerate(zip(weights, sums))
        ]
        columns = [top * EXP2_SCALE + jnp.log2(total) for top, total in zip(tops, sums)]
        head_lane = lax.broadcasted_iota(jnp.int32, (tall, 128), 1)
        lse = jnp.zeros((tall, 128), jnp.float32)
        for head in range(kv_heads):
            for j in range(group):
                lse = jnp.where(
                    head_lane == head * group + j, columns[head][j * tall:(j + 1) * tall], lse
                )
        return mixed, lse

    def own_part():
        key_lane = lax.broadcasted_iota(jnp.int32, (group * slots, rows), 1)
        seen = key_lane <= jnp.concatenate([row_place] * group, axis=0)
        mixed, lse = attend(q_own, slots, seen)
        lse_all[...] = jnp.full_like(lse_all, MASKED)
        lse_all[ctx] = lse
        for head in range(kv_heads):
            for j in range(group):
                part_all[ctx, :, lanes(head * group + j)] = mixed[head][
                    j * slots:(j + 1) * slots
                ]

    def put_row(place, picked):
        for expert in range(n_ep):
            out_rows[expert, place * CAP:(place + 1) * CAP] = picked[
                expert * CAP:(expert + 1) * CAP
            ].astype(jnp.bfloat16)

    def send_rows():
        others(lambda other: row_copy(other, me).start())
        in_rows[me] = out_rows[ep]

    part_all[...] = jnp.zeros_like(part_all)
    q_all[...] = jnp.zeros_like(q_all)

    @pl.when(ctx == 0)
    def _():
        with scope("b_own0"):
            for copy in own_copies:
                copy.wait()
            own_part()
            for place in range(places):
                put_row(place, part_all[0, :, lanes(place)])

    with scope("c_barrier"):
        pl.semaphore_wait(barrier, n - 1 + n_tp - 1)

    with scope("d_qsend"):
        lower(lambda other: q_copy(ctx, other).start())

    @pl.when(ctx == 0)
    def _():
        with scope("e_rows0"):
            send_rows()
            push_own(range(kv_heads - 1))

    @pl.when(ctx > 0)
    def _():
        with scope("f_own"):
            for copy in own_copies:
                copy.wait()
            push_own(range(kv_heads - 1))
            own_part()

    query_offset = lax.broadcasted_iota(jnp.int32, (rows, rows), 0)
    key_offset = lax.broadcasted_iota(jnp.int32, (rows, rows), 1)

    def scores(block, head):
        stacked = jnp.concatenate(
            [q_ref[:, lanes(head * group + j)] for j in range(group)], axis=0
        )
        return lax.dot_general(
            stacked, kv[block, head, 0], (((1,), (1,)), ((), ())),
            preferred_element_type=jnp.float32,
        )

    def mix(weights, block, head):
        return jnp.dot(
            weights.astype(jnp.bfloat16), kv[block, head, 1], preferred_element_type=jnp.float32
        )

    with scope("g_own_block"):
        visible = jnp.concatenate([query_offset >= key_offset] * group, axis=0)
        for head in range(kv_heads):
            raw = jnp.where(visible, scores(ctx, head), MASKED)
            top = jnp.broadcast_to(jnp.max(raw, axis=1, keepdims=True), raw.shape)
            weights = jnp.exp2((raw - top) * EXP2_SCALE)
            row_max[head] = top
            totals[head] = jnp.broadcast_to(
                jnp.sum(weights, axis=1, keepdims=True), weights.shape
            )
            acc[head] = mix(weights, ctx, head)

    def process(block, head):
        raw = scores(block, head)
        old_max = row_max[head]
        new_max = jnp.maximum(old_max, jnp.max(raw, axis=1, keepdims=True))
        factor = jnp.exp2((old_max - new_max) * EXP2_SCALE)
        weights = jnp.exp2((raw - new_max) * EXP2_SCALE)
        row_max[head] = new_max
        totals[head] = totals[head] * factor + jnp.sum(weights, axis=1, keepdims=True)
        acc[head] = acc[head] * factor + mix(weights, block, head)

    def process_block(step):
        @pl.when(ctx >= step)
        def _():
            for head in range(kv_heads):
                process(ctx - step, head)

    @pl.when(ctx < last)
    def _():
        with scope("h_qwait"):
            upper(lambda other: q_copy(other, other).wait_recv())
        with scope("i_qpart"):
            for other in range(n_ctx):
                @pl.when(other > ctx)
                def _():
                    q_all[other * live:(other + 1) * live, :] = q_in[other].astype(jnp.float32)

            tall = n_ctx * live
            mixed, lse = attend(q_all, tall, None)
            for other in range(n_ctx):
                lse_out[other, :live] = lse[other * live:(other + 1) * live]
                for place in range(places):
                    first = place % group * tall + other * live
                    part_out[other, :, lanes(place)] = mixed[place // group][
                        first:first + live
                    ].astype(jnp.bfloat16)

        with scope("j_give"):
            def give_back(other):
                for copy in back_copies(ctx, other):
                    copy.start()

            upper(give_back)
            push_own([kv_heads - 1])

    with scope("k_relay"):
        relay(ctx - 1, [0])

    peer = {"tp": n_tp - 1 - tp}

    def gate(indices, wide_ref, part, part_in, score, score_in, sent, got, score_sem):
        for at, index in enumerate(indices):
            dense = in_rows[index].astype(jnp.float32)
            for place in range(places):
                wide_ref[at * CAP:(at + 1) * CAP, lanes(place)] = dense[
                    place * CAP:(place + 1) * CAP
                ]
        wide = wide_ref[...]
        members = wide.astype(jnp.bfloat16)
        own_score = jnp.sum(wide * router_ref[...].astype(jnp.float32), axis=1, keepdims=True)
        score[...] = jnp.broadcast_to(own_score, score.shape).astype(jnp.bfloat16)
        copies = [pltpu.make_async_remote_copy(
            src_ref=score, dst_ref=score_in,
            send_sem=score_sem.at[0], recv_sem=score_sem.at[1],
            device_id=peer, device_id_type=MESH,
        )]
        copies[0].start()
        chunk_count, _, double_width = part.shape
        width = double_width // 2
        for chunk in range(chunk_count):
            span = slice(chunk * width, (chunk + 1) * width)
            for side, weight in enumerate((wg, wu)):
                part[chunk, :, side * width:(side + 1) * width] = jnp.dot(
                    members, weight[:, span], preferred_element_type=jnp.float32
                ).astype(jnp.bfloat16)
            copy = pltpu.make_async_remote_copy(
                src_ref=part.at[chunk], dst_ref=part_in.at[chunk],
                send_sem=sent.at[chunk], recv_sem=got.at[chunk],
                device_id=peer, device_id_type=MESH,
            )
            copy.start()
            copies.append(copy)
        return copies

    def activate(copies, part, part_in, score, score_in, hidden):
        copies[0].wait()
        gain = jax.nn.sigmoid(
            score[:, :1].astype(jnp.float32) + score_in[:, :1].astype(jnp.float32)
        )
        width = part.shape[2] // 2
        for chunk, copy in enumerate(copies[1:]):
            copy.wait()
            both = part[chunk].astype(jnp.float32) + part_in[chunk].astype(jnp.float32)
            gate_part = gain * both[:, :width]
            up_part = gain * both[:, width:]
            hidden[:, chunk * width:(chunk + 1) * width] = (
                gate_part * jax.nn.sigmoid(gate_part) * up_part
            ).astype(jnp.bfloat16)

    def down(indices, hidden):
        for start, size in tiles_of(features, 512):
            product = jnp.dot(
                hidden[...], wd[:, start:start + size], preferred_element_type=jnp.float32
            )
            for at, index in enumerate(indices):
                for place in range(start // HEAD_WIDTH, (start + size) // HEAD_WIDTH):
                    lane = place * HEAD_WIDTH - start
                    down_out[index, place * CAP:(place + 1) * CAP] = product[
                        at * CAP:(at + 1) * CAP, lane:lane + HEAD_WIDTH
                    ].astype(jnp.bfloat16)

    def keep_own():
        down_in[me] = down_out[me]

    first = [index for index in range(n) if index % n_ctx == 0]
    later = [index for index in range(n) if index % n_ctx != 0]
    exchange_a = (part_a, part_in_a, score_a, score_in_a)
    exchange_b = (part_b, part_in_b, score_b, score_in_b)

    with scope("l_rows_a"):
        in_copies[2].wait()
        w_copies[0].wait()
        w_copies[1].wait()
        first_owners(lambda other: row_copy(other, other).wait_recv())
    with scope("m_gate_a"):
        copies_a = gate(first, members_a, *exchange_a, a_send, a_recv, a_score)
    with scope("n_relay"):
        relay(ctx - 1, [1])

    @pl.when(ctx > 0)
    def _():
        with scope("o_takeback"):
            def take_back(other):
                for copy in back_copies(other, other):
                    copy.wait_recv()

            lower(take_back)
        with scope("p_combine"):
            for other in range(last):
                @pl.when(other < ctx)
                def _():
                    part_all[other, :live] = part_got[other].astype(jnp.float32)
                    lse_all[other, :live] = lse_in[other, :live]

            peak = jnp.max(lse_all[...], axis=0)
            shares = [jnp.exp2(lse_all[other] - peak) for other in range(n_ctx)]
            share_total = functools.reduce(jnp.add, shares)
            shares = [share / share_total for share in shares]
            for place in range(places):
                put_row(place, functools.reduce(jnp.add, [
                    shares[other][:, place:place + 1] * part_all[other, :, lanes(place)]
                    for other in range(n_ctx)
                ]))
        with scope("q_rows"):
            send_rows()

    with scope("r_relay"):
        relay(ctx - 1, range(2, kv_heads))
    with scope("s_down_a"):
        w_copies[2].wait()
        activate(copies_a, *exchange_a, hidden_a)
        down(first, hidden_a)
        first_owners(lambda other: down_copy(other, me).start())
        pl.when(ctx == 0)(keep_own)
    with scope("t_block1"):
        process_block(1)
    with scope("u_relay"):
        relay(ctx - 2, range(2))
    with scope("v_rows_b"):
        later_owners(lambda other: row_copy(other, other).wait_recv())
    with scope("w_gate_b"):
        copies_b = gate(later, members_b, *exchange_b, b_send, b_recv, b_score)
    with scope("x_relay"):
        relay(ctx - 2, range(2, kv_heads))
    with scope("xa_block2"):
        process_block(2)
    with scope("xb_down_b"):
        activate(copies_b, *exchange_b, hidden_b)
        down(later, hidden_b)
        later_owners(lambda other: down_copy(other, me).start())
        pl.when(ctx > 0)(keep_own)

    def visit(step, carry):
        @pl.when(ctx >= step)
        def _():
            for head in range(kv_heads):
                relay(ctx - step, [head])
                process(ctx - step, head)

        return carry

    with scope("xc_visit"):
        lax.fori_loop(3, n_ctx, visit, 0)

    with scope("xd_norm"):
        for head in range(kv_heads):
            normed = (acc[head] / totals[head]).astype(jnp.bfloat16)
            for j in range(group):
                att[:, lanes(head * group + j)] = normed[j * rows:(j + 1) * rows]
        returned[...] = jnp.zeros_like(returned)

    with scope("xe_sent"):
        others(lambda other: row_copy(other, me).wait_send())
        lower(lambda other: q_copy(ctx, other).wait_send())

        def sent_back(other):
            for copy in back_copies(ctx, other):
                copy.wait_send()

        upper(sent_back)

        def drain(step, carry):
            @pl.when((ctx < last) & (ctx >= step))
            def _():
                for head in range(kv_heads):
                    kv_copy(ctx - step, head).wait_send()

            return carry

        lax.fori_loop(0, n_ctx, drain, 0)

    with scope("xf_downwait"):
        others(lambda other: down_copy(other, other).wait_recv())
    with scope("xg_final"):
        for expert in range(n_ep):
            total = down_in[expert * n_ctx].astype(jnp.float32)
            for index in range(1, n_ctx):
                total = total + down_in[expert * n_ctx + index].astype(jnp.float32)
            total = total.astype(jnp.bfloat16).astype(jnp.float32)
            for place in range(places):
                returned[expert * CAP:(expert + 1) * CAP, lanes(place)] = total[
                    place * CAP:(place + 1) * CAP
                ]
        for start, size in tiles_of(features, 512):
            routed = lax.dot_general(
                spread, returned[:, start:start + size].astype(jnp.bfloat16),
                (((0,), (0,)), ((), ())), preferred_element_type=jnp.float32,
            )
            out_ref[0, :, start:start + size] = (
                att[:, start:start + size].astype(jnp.float32) + routed
            ).astype(jnp.bfloat16)
    others(lambda other: down_copy(other, me).wait_send())


def shards(queries, keys, values, expert_ids, router, w_gate, w_up, w_down):
    n_ctx, n_ep, n_tp = (lax.axis_size(axis) for axis in ("ctx", "ep", "tp"))
    n = n_ctx * n_ep
    _, rows, features = queries.shape
    kv_width = keys.shape[2]
    kv_heads = kv_width // HEAD_WIDTH
    group = features // kv_width
    hidden_width = w_gate.shape[2]
    chunk_width = min(hidden_width, 256)
    chunks = hidden_width // chunk_width
    dense = features // HEAD_WIDTH * CAP
    live = n_ep * CAP
    slots = padded(live)
    bf16, f32 = jnp.bfloat16, jnp.float32
    hbm = pl.BlockSpec(memory_space=pltpu.HBM)
    dma = pltpu.SemaphoreType.DMA

    def batch(count):
        return [
            pltpu.VMEM((count, features), f32),
            pltpu.VMEM((chunks, count, 2 * chunk_width), bf16),
            pltpu.VMEM((chunks, count, 2 * chunk_width), bf16),
            pltpu.VMEM((count, 128), bf16),
            pltpu.VMEM((count, 128), bf16),
            pltpu.VMEM((count, hidden_width), bf16),
        ]

    return pl.pallas_call(
        functools.partial(kernel, n_ctx, n_ep, n_tp),
        out_shape=pltpu.VMEM(queries.shape, bf16),
        in_specs=[hbm] * 8,
        out_specs=pl.BlockSpec(memory_space=pltpu.VMEM),
        scratch_shapes=[
            pltpu.VMEM((1, rows), jnp.int32),
            pltpu.VMEM((1, features), bf16),
            pltpu.VMEM((rows, features), bf16),
            pltpu.VMEM(w_gate.shape[1:], bf16),
            pltpu.VMEM(w_up.shape[1:], bf16),
            pltpu.VMEM(w_down.shape[1:], bf16),
            pltpu.VMEM((n_ctx, kv_heads, 2, rows, HEAD_WIDTH), bf16),
            pltpu.VMEM((kv_heads, group * rows, HEAD_WIDTH), f32),
            pltpu.VMEM((kv_heads, group * rows, HEAD_WIDTH), f32),
            pltpu.VMEM((kv_heads, group * rows, HEAD_WIDTH), f32),
            pltpu.VMEM((rows, features), bf16),
            pltpu.VMEM((slots, features), f32),
            pltpu.VMEM((live, features), bf16),
            pltpu.VMEM((n_ctx, live, features), bf16),
            pltpu.VMEM((n_ctx * live, features), f32),
            pltpu.VMEM((n_ctx, live, features), bf16),
            pltpu.VMEM((n_ctx, live, features), bf16),
            pltpu.VMEM((n_ctx, slots, features), f32),
            pltpu.VMEM((n_ctx, slots, 128), f32),
            pltpu.VMEM((n_ctx, slots, 128), f32),
            pltpu.VMEM((n_ctx, slots, 128), f32),
            pltpu.VMEM((n_ep, dense, HEAD_WIDTH), bf16),
            pltpu.VMEM((n, dense, HEAD_WIDTH), bf16),
            *batch(n_ep * CAP),
            *batch((n - n_ep) * CAP),
            pltpu.VMEM((n, dense, HEAD_WIDTH), bf16),
            pltpu.VMEM((n, dense, HEAD_WIDTH), bf16),
            pltpu.VMEM((slots, features), f32),
            dma((3,)),
            dma((kv_heads, 2)),
            dma((3,)),
            dma((n_ctx, kv_heads)),
            dma((n_ctx, kv_heads)),
            dma((n,)),
            dma((n,)),
            dma((chunks,)),
            dma((chunks,)),
            dma((2,)),
            dma((chunks,)),
            dma((chunks,)),
            dma((2,)),
            dma((n,)),
            dma((n,)),
            dma((n_ctx,)),
            dma((n_ctx,)),
            dma((n_ctx,)),
            dma((n_ctx,)),
            dma((n_ctx,)),
            dma((n_ctx,)),
        ],
        compiler_params=pltpu.CompilerParams(
            collective_id=0, has_side_effects=True, vmem_limit_bytes=60 * 1024 * 1024
        ),
    )(
        expert_ids.reshape(1, rows), router.reshape(1, features), queries, keys, values,
        w_gate, w_up, w_down,
    )


def solution(mesh):
    placed = (
        P(("groups", "ep"), "ctx", "tp"),
        P(("groups", "ep"), "ctx", "tp"),
        P(("groups", "ep"), "ctx", "tp"),
        P(("groups", "ep"), "ctx", None),
        P("tp", "ep"),
        P("ep", "tp", "ctx"),
        P("ep", "tp", "ctx"),
        P("ep", "ctx", "tp"),
    )
    return jax.shard_map(
        shards,
        mesh=mesh,
        in_specs=placed,
        out_specs=P(("groups", "ep"), "ctx", "tp"),
        check_vma=False,
    )
```

time: 29.7 us -> 29.6 us (level)
  no operation moved by 1% of the time
where the time goes in v2:
time: 29.6 us; the launch traced here: 29.4 us
  Pallas kernels  28.6 us (97%)
  local copies, waits for them, and re-layouts  0.84 us (3%)
    pallas_call x1, Pallas kernels, shards(): pl.pallas_call(functools.partial(kernel, n_ctx, n_ep, n_tp), out_shape=pl...  28.6 us
    unnamed x1, local copies, waits for them, and re-layouts  0.84 us

profile of v2, /device:TPU:24, one launch (start us, length us, event | category | flops | bytes accessed | tf_op | source)
XLA Modules:
  0.0 29.4 jit_solution(10167557152185792273)
XLA Ops:
  0.0 28.6 %shard_map.82 = bf16[1,128,2560]{2,1,0:T(8,128)(2,1)S(1)} custom-call(s32[1,128]{1,0:T(1,128)} %bitcast.3, bf16[1,2560]{1,0:T(2,128)(2,1)} %bitcast.2, bf16[1,128,2560]{2,1,0:T(8,128)(2,1)} %q_hbm.1, bf16[1,128,512]{2,1,0:T(8,128)(2,1)} %k_hbm.1, bf16[1,128,512]{2,1,0:T(8,128)(2,1)} %v_hbm.1, bf16[1,2560,1024]{2,1,0:T(8,128)(2,1)} %wg_hbm.1, ...), custom_call_target="tpu_custom_call" | custom-call | tf_op jit(solution)/shard_map/pallas_call | solution.py:612
  28.6 0.8 %copy.10 = bf16[1,128,2560]{2,1,0:T(8,128)(2,1)} copy(bf16[1,128,2560]{2,1,0:T(8,128)(2,1)S(1)} %shard_map.82) | data formatting | bytes 1310720

commit v3 on v2

--- a/solution.py
+++ b/solution.py
@@ -37,14 +37,14 @@
     n_ctx, n_ep, n_tp,
     ids_hbm, router_hbm, q_hbm, k_hbm, v_hbm, wg_hbm, wu_hbm, wd_hbm,
     out_ref,
-    ids_ref, router_ref, q_ref, wg, wu, wd, kv, acc, row_max, totals, att,
-    q_own, q_out, q_in, q_all, part_out, part_got, part_all, lse_out, lse_in, lse_all,
+    ids_ref, router_ref, q_ref, wgu, wd, kv, acc, row_max, totals, att,
+    q_own, q_out, q_in, q_pad, part_out, part_got, part_all, lse_out, lse_in, lse_all,
     out_rows, in_rows,
-    members_a, part_a, part_in_a, score_a, score_in_a, hidden_a,
-    members_b, part_b, part_in_b, score_b, score_in_b, hidden_b,
+    members_a, part_a, part_in_a, hidden_a,
+    members_b, part_b, part_in_b, hidden_b,
     down_out, down_in, returned,
     in_sem, own_sem, w_sem, kv_send, kv_recv, row_send, row_recv,
-    a_send, a_recv, a_score, b_send, b_recv, b_score,
+    a_send, a_recv, b_send, b_recv,
     down_send, down_recv, q_send, q_recv, back_send, back_recv, lse_send, lse_recv,
 ):
     ctx = lax.axis_index("ctx")
@@ -71,16 +71,19 @@
     ]
     own_copies = [
         pltpu.make_async_copy(
-            src.at[0, :, lanes(head)], kv.at[ctx, head, which], own_sem.at[head, which]
+            src.at[0, :, lanes(head)], kv.at[ctx, head, which], own_sem
         )
         for head in range(kv_heads)
         for which, src in enumerate((k_hbm, v_hbm))
     ]
     w_copies = [
-        pltpu.make_async_copy(src.at[0], dst, w_sem.at[index])
-        for index, (src, dst) in enumerate(((wg_hbm, wg), (wu_hbm, wu), (wd_hbm, wd)))
+        pltpu.make_async_copy(src.at[0], dst, sem)
+        for src, dst, sem in (
+            (wg_hbm, wgu.at[0], w_sem.at[0]), (wu_hbm, wgu.at[1], w_sem.at[0]),
+            (wd_hbm, wd, w_sem.at[1]),
+        )
     ]
-    for copy in in_copies[:2] + own_copies + in_copies[2:] + w_copies:
+    for copy in in_copies[:2] + own_copies + in_copies[2:]:
         copy.start()
 
     barrier = pltpu.get_barrier_semaphore()
@@ -100,10 +103,22 @@
             barrier, inc=1, device_id={"tp": (tp + step) % n_tp}, device_id_type=MESH
         )
 
+    peer = {"tp": n_tp - 1 - tp}
+
+    def settled(ref, sem):
+        return pltpu.make_async_remote_copy(
+            src_ref=ref, dst_ref=ref, send_sem=sem, recv_sem=sem,
+            device_id=peer, device_id_type=MESH,
+        )
+
+    def by_ctx(body):
+        for index in range(n_ctx):
+            pl.when(ctx == index)(functools.partial(body, index))
+
     def kv_copy(block, head):
         return pltpu.make_async_remote_copy(
             src_ref=kv.at[block, head], dst_ref=kv.at[block, head],
-            send_sem=kv_send.at[block, head], recv_sem=kv_recv.at[block, head],
+            send_sem=kv_send, recv_sem=kv_recv.at[block, head],
             device_id={"ctx": ctx + 1}, device_id_type=MESH,
         )
 
@@ -127,7 +142,7 @@
     def q_copy(source, target):
         return pltpu.make_async_remote_copy(
             src_ref=q_out, dst_ref=q_in.at[source],
-            send_sem=q_send.at[target], recv_sem=q_recv.at[source],
+            send_sem=q_send, recv_sem=q_recv.at[source],
             device_id={"ctx": target}, device_id_type=MESH,
         )
 
@@ -135,7 +150,7 @@
         return [
             pltpu.make_async_remote_copy(
                 src_ref=out.at[target], dst_ref=into.at[source],
-                send_sem=sent.at[target], recv_sem=got.at[source],
+                send_sem=sent, recv_sem=got,
                 device_id={"ctx": target}, device_id_type=MESH,
             )
             for out, into, sent, got in (
@@ -147,12 +162,13 @@
     def to_index(other, out, into, sent, got, source):
         return pltpu.make_async_remote_copy(
             src_ref=out, dst_ref=into.at[source],
-            send_sem=sent.at[other], recv_sem=got.at[source],
+            send_sem=sent, recv_sem=got,
             device_id={"ep": other // n_ctx, "ctx": other % n_ctx}, device_id_type=MESH,
         )
 
     def row_copy(other, source):
-        return to_index(other, out_rows.at[other // n_ctx], in_rows, row_send, row_recv, source)
+        got = row_recv.at[jnp.where(ctx == 0, 0, 1)]
+        return to_index(other, out_rows.at[other // n_ctx], in_rows, row_send, got, source)
 
     def down_copy(other, source):
         return to_index(other, down_out.at[other], down_in, down_send, down_recv, source)
@@ -199,8 +215,9 @@
 
         each(n, one)
 
+    with scope("a_ids"):
+        in_copies[0].wait()
     with scope("a_pick"):
-        in_copies[0].wait()
         ids = ids_ref[...]
         slot_row = lax.broadcasted_iota(jnp.int32, (slots, rows), 0)
         choose = jnp.where(ids == slot_row, 1.0, 0.0)
@@ -218,6 +235,8 @@
             jnp.where(target_row == slot_row, lane_row, 0), axis=1, keepdims=True
         )
         in_copies[1].wait()
+        for copy in w_copies:
+            copy.start()
         for start, size in tiles_of(features, 512):
             picked = jnp.dot(
                 spread, q_ref[:, start:start + size], preferred_element_type=jnp.float32
@@ -256,6 +275,9 @@
                 )
         return mixed, lse
 
+    def own_landed():
+        pltpu.make_async_copy(kv.at[ctx], kv.at[ctx], own_sem).wait()
+
     def own_part():
         key_lane = lax.broadcasted_iota(jnp.int32, (group * slots, rows), 1)
         seen = key_lane <= jnp.concatenate([row_place] * group, axis=0)
@@ -279,13 +301,12 @@
         in_rows[me] = out_rows[ep]
 
     part_all[...] = jnp.zeros_like(part_all)
-    q_all[...] = jnp.zeros_like(q_all)
+    q_pad[...] = jnp.zeros_like(q_pad)
 
     @pl.when(ctx == 0)
     def _():
         with scope("b_own0"):
-            for copy in own_copies:
-                copy.wait()
+            own_landed()
             own_part()
             for place in range(places):
                 put_row(place, part_all[0, :, lanes(place)])
@@ -300,13 +321,12 @@
     def _():
         with scope("e_rows0"):
             send_rows()
-            push_own(range(kv_heads - 1))
+            push_own(range(2))
 
     @pl.when(ctx > 0)
     def _():
         with scope("f_own"):
-            for copy in own_copies:
-                copy.wait()
+            own_landed()
             push_own(range(kv_heads - 1))
             own_part()
 
@@ -357,38 +377,35 @@
 
     @pl.when(ctx < last)
     def _():
-        with scope("h_qwait"):
-            upper(lambda other: q_copy(other, other).wait_recv())
-        with scope("i_qpart"):
-            for other in range(n_ctx):
-                @pl.when(other > ctx)
-                def _():
-                    q_all[other * live:(other + 1) * live, :] = q_in[other].astype(jnp.float32)
-
-            tall = n_ctx * live
-            mixed, lse = attend(q_all, tall, None)
-            for other in range(n_ctx):
-                lse_out[other, :live] = lse[other * live:(other + 1) * live]
-                for place in range(places):
-                    first = place % group * tall + other * live
-                    part_out[other, :, lanes(place)] = mixed[place // group][
-                        first:first + live
-                    ].astype(jnp.bfloat16)
-
-        with scope("j_give"):
-            def give_back(other):
-                for copy in back_copies(ctx, other):
-                    copy.start()
-
-            upper(give_back)
-            push_own([kv_heads - 1])
+        def answer(step, carry):
+            other = ctx + step
+
+            @pl.when(other <= last)
+            def _():
+                with scope("h_qwait"):
+                    q_copy(other, other).wait_recv()
+                with scope("i_qpart"):
+                    q_pad[:live] = q_in[other].astype(jnp.float32)
+                    mixed, lse = attend(q_pad, slots, None)
+                    lse_out[other] = lse[:live]
+                    for place in range(places):
+                        first = place % group * slots
+                        part_out[other, :, lanes(place)] = mixed[place // group][
+                            first:first + live
+                        ].astype(jnp.bfloat16)
+                    for copy in back_copies(ctx, other):
+                        copy.start()
+
+            return carry
+
+        lax.fori_loop(1, n_ctx, answer, 0)
+        pl.when(ctx == 0)(lambda: push_own(range(2, kv_heads)))
+        pl.when(ctx > 0)(lambda: push_own([kv_heads - 1]))
 
     with scope("k_relay"):
-        relay(ctx - 1, [0])
-
-    peer = {"tp": n_tp - 1 - tp}
-
-    def gate(indices, wide_ref, part, part_in, score, score_in, sent, got, score_sem):
+        pl.when(ctx > 1)(lambda: relay(ctx - 1, [0]))
+
+    def gate(indices, wide_ref, part, part_in, sent, got):
         for at, index in enumerate(indices):
             dense = in_rows[index].astype(jnp.float32)
             for place in range(places):
@@ -398,42 +415,38 @@
         wide = wide_ref[...]
         members = wide.astype(jnp.bfloat16)
         own_score = jnp.sum(wide * router_ref[...].astype(jnp.float32), axis=1, keepdims=True)
-        score[...] = jnp.broadcast_to(own_score, score.shape).astype(jnp.bfloat16)
-        copies = [pltpu.make_async_remote_copy(
-            src_ref=score, dst_ref=score_in,
-            send_sem=score_sem.at[0], recv_sem=score_sem.at[1],
-            device_id=peer, device_id_type=MESH,
-        )]
-        copies[0].start()
-        chunk_count, _, double_width = part.shape
+        chunks, _, double_width = part.shape
         width = double_width // 2
-        for chunk in range(chunk_count):
-            span = slice(chunk * width, (chunk + 1) * width)
-            for side, weight in enumerate((wg, wu)):
-                part[chunk, :, side * width:(side + 1) * width] = jnp.dot(
-                    members, weight[:, span], preferred_element_type=jnp.float32
-                ).astype(jnp.bfloat16)
-            copy = pltpu.make_async_remote_copy(
+        for chunk in range(chunks):
+            if chunk == 0:
+                part[0] = jnp.broadcast_to(own_score, part.shape[1:]).astype(jnp.bfloat16)
+            else:
+                span = slice((chunk - 1) * width, chunk * width)
+                for side in range(2):
+                    part[chunk, :, side * width:(side + 1) * width] = jnp.dot(
+                        members, wgu[side, :, span], preferred_element_type=jnp.float32
+                    ).astype(jnp.bfloat16)
+            which = chunk // (chunks - 1)
+            pltpu.make_async_remote_copy(
                 src_ref=part.at[chunk], dst_ref=part_in.at[chunk],
-                send_sem=sent.at[chunk], recv_sem=got.at[chunk],
+                send_sem=sent, recv_sem=got.at[which],
                 device_id=peer, device_id_type=MESH,
-            )
-            copy.start()
-            copies.append(copy)
-        return copies
-
-    def activate(copies, part, part_in, score, score_in, hidden):
-        copies[0].wait()
+            ).start()
+
+    def activate(part, part_in, sent, got, hidden):
+        chunks = part.shape[0]
+        width = part.shape[2] // 2
+        settled(part_in.at[pl.ds(0, chunks - 1)], got.at[0]).wait_recv()
         gain = jax.nn.sigmoid(
-            score[:, :1].astype(jnp.float32) + score_in[:, :1].astype(jnp.float32)
-        )
-        width = part.shape[2] // 2
-        for chunk, copy in enumerate(copies[1:]):
-            copy.wait()
+            part[0, :, :1].astype(jnp.float32) + part_in[0, :, :1].astype(jnp.float32)
+        )
+        for chunk in range(1, chunks):
+            if chunk == chunks - 1:
+                settled(part_in.at[chunk], got.at[1]).wait_recv()
             both = part[chunk].astype(jnp.float32) + part_in[chunk].astype(jnp.float32)
             gate_part = gain * both[:, :width]
             up_part = gain * both[:, width:]
-            hidden[:, chunk * width:(chunk + 1) * width] = (
+            hidden[:, (chunk - 1) * width:chunk * width] = (
                 gate_part * jax.nn.sigmoid(gate_part) * up_part
             ).astype(jnp.bfloat16)
 
@@ -454,33 +467,42 @@
 
     first = [index for index in range(n) if index % n_ctx == 0]
     later = [index for index in range(n) if index % n_ctx != 0]
-    exchange_a = (part_a, part_in_a, score_a, score_in_a)
-    exchange_b = (part_b, part_in_b, score_b, score_in_b)
+    exchange_a = (part_a, part_in_a, a_send, a_recv)
+    exchange_b = (part_b, part_in_b, b_send, b_recv)
 
     with scope("l_rows_a"):
         in_copies[2].wait()
-        w_copies[0].wait()
-        w_copies[1].wait()
-        first_owners(lambda other: row_copy(other, other).wait_recv())
+        pltpu.make_async_copy(wgu, wgu, w_sem.at[0]).wait()
+
+        @pl.when(ctx == 0)
+        def _():
+            if n_ep > 1:
+                settled(in_rows.at[pl.ds(0, n_ep - 1)], row_recv.at[0]).wait_recv()
+
+        @pl.when(ctx > 0)
+        def _():
+            settled(in_rows.at[pl.ds(0, n_ep)], row_recv.at[0]).wait_recv()
     with scope("m_gate_a"):
-        copies_a = gate(first, members_a, *exchange_a, a_send, a_recv, a_score)
+        gate(first, members_a, *exchange_a)
     with scope("n_relay"):
-        relay(ctx - 1, [1])
+        pl.when(ctx == 1)(lambda: relay(ctx - 1, [0]))
+        pl.when(ctx > 1)(lambda: relay(ctx - 1, range(1, kv_heads - 1)))
 
     @pl.when(ctx > 0)
     def _():
         with scope("o_takeback"):
-            def take_back(other):
-                for copy in back_copies(other, other):
-                    copy.wait_recv()
-
-            lower(take_back)
+            def take_back(count):
+                if count:
+                    settled(part_got.at[pl.ds(0, count)], back_recv).wait_recv()
+                    settled(lse_in.at[pl.ds(0, count)], lse_recv).wait_recv()
+
+            by_ctx(take_back)
         with scope("p_combine"):
             for other in range(last):
                 @pl.when(other < ctx)
                 def _():
                     part_all[other, :live] = part_got[other].astype(jnp.float32)
-                    lse_all[other, :live] = lse_in[other, :live]
+                    lse_all[other, :live] = lse_in[other]
 
             peak = jnp.max(lse_all[...], axis=0)
             shares = [jnp.exp2(lse_all[other] - peak) for other in range(n_ctx)]
@@ -495,10 +517,11 @@
             send_rows()
 
     with scope("r_relay"):
-        relay(ctx - 1, range(2, kv_heads))
+        pl.when(ctx == 1)(lambda: relay(ctx - 1, range(1, kv_heads)))
+        pl.when(ctx > 1)(lambda: relay(ctx - 1, [kv_heads - 1]))
     with scope("s_down_a"):
         w_copies[2].wait()
-        activate(copies_a, *exchange_a, hidden_a)
+        activate(*exchange_a, hidden_a)
         down(first, hidden_a)
         first_owners(lambda other: down_copy(other, me).start())
         pl.when(ctx == 0)(keep_own)
@@ -507,15 +530,22 @@
     with scope("u_relay"):
         relay(ctx - 2, range(2))
     with scope("v_rows_b"):
-        later_owners(lambda other: row_copy(other, other).wait_recv())
+        @pl.when(ctx == 0)
+        def _():
+            settled(in_rows.at[pl.ds(0, n - n_ep)], row_recv.at[1]).wait_recv()
+
+        @pl.when(ctx > 0)
+        def _():
+            settled(in_rows.at[pl.ds(0, n - n_ep - 1)], row_recv.at[1]).wait_recv()
+
     with scope("w_gate_b"):
-        copies_b = gate(later, members_b, *exchange_b, b_send, b_recv, b_score)
+        gate(later, members_b, *exchange_b)
     with scope("x_relay"):
         relay(ctx - 2, range(2, kv_heads))
     with scope("xa_block2"):
         process_block(2)
     with scope("xb_down_b"):
-        activate(copies_b, *exchange_b, hidden_b)
+        activate(*exchange_b, hidden_b)
         down(later, hidden_b)
         later_owners(lambda other: down_copy(other, me).start())
         pl.when(ctx > 0)(keep_own)
@@ -540,27 +570,22 @@
         returned[...] = jnp.zeros_like(returned)
 
     with scope("xe_sent"):
-        others(lambda other: row_copy(other, me).wait_send())
-        lower(lambda other: q_copy(ctx, other).wait_send())
-
-        def sent_back(other):
-            for copy in back_copies(ctx, other):
-                copy.wait_send()
-
-        upper(sent_back)
-
-        def drain(step, carry):
-            @pl.when((ctx < last) & (ctx >= step))
-            def _():
-                for head in range(kv_heads):
-                    kv_copy(ctx - step, head).wait_send()
-
-            return carry
-
-        lax.fori_loop(0, n_ctx, drain, 0)
+        settled(in_rows.at[pl.ds(0, n - 1)], row_send).wait_send()
+        settled(part_a, a_send).wait_send()
+        settled(part_b, b_send).wait_send()
+
+        def drain(index):
+            if index:
+                settled(q_in.at[pl.ds(0, index)], q_send).wait_send()
+            if index < last:
+                settled(part_out.at[pl.ds(0, last - index)], back_send).wait_send()
+                settled(lse_out.at[pl.ds(0, last - index)], lse_send).wait_send()
+                settled(kv.at[pl.ds(0, index + 1)], kv_send).wait_send()
+
+        by_ctx(drain)
 
     with scope("xf_downwait"):
-        others(lambda other: down_copy(other, other).wait_recv())
+        settled(down_in.at[pl.ds(0, n - 1)], down_recv).wait_recv()
     with scope("xg_final"):
         for expert in range(n_ep):
             total = down_in[expert * n_ctx].astype(jnp.float32)
@@ -579,7 +604,8 @@
             out_ref[0, :, start:start + size] = (
                 att[:, start:start + size].astype(jnp.float32) + routed
             ).astype(jnp.bfloat16)
-    others(lambda other: down_copy(other, me).wait_send())
+    with scope("xh_sent"):
+        settled(down_out.at[pl.ds(0, n - 1)], down_send).wait_send()
 
 
 def shards(queries, keys, values, expert_ids, router, w_gate, w_up, w_down):
@@ -602,10 +628,8 @@
     def batch(count):
         return [
             pltpu.VMEM((count, features), f32),
-            pltpu.VMEM((chunks, count, 2 * chunk_width), bf16),
-            pltpu.VMEM((chunks, count, 2 * chunk_width), bf16),
-            pltpu.VMEM((count, 128), bf16),
-            pltpu.VMEM((count, 128), bf16),
+            pltpu.VMEM((chunks + 1, count, 2 * chunk_width), bf16),
+            pltpu.VMEM((chunks + 1, count, 2 * chunk_width), bf16),
             pltpu.VMEM((count, hidden_width), bf16),
         ]
 
@@ -618,8 +642,7 @@
             pltpu.VMEM((1, rows), jnp.int32),
             pltpu.VMEM((1, features), bf16),
             pltpu.VMEM((rows, features), bf16),
-            pltpu.VMEM(w_gate.shape[1:], bf16),
-            pltpu.VMEM(w_up.shape[1:], bf16),
+            pltpu.VMEM((2, *w_gate.shape[1:]), bf16),
             pltpu.VMEM(w_down.shape[1:], bf16),
             pltpu.VMEM((n_ctx, kv_heads, 2, rows, HEAD_WIDTH), bf16),
             pltpu.VMEM((kv_heads, group * rows, HEAD_WIDTH), f32),
@@ -629,12 +652,12 @@
             pltpu.VMEM((slots, features), f32),
             pltpu.VMEM((live, features), bf16),
             pltpu.VMEM((n_ctx, live, features), bf16),
-            pltpu.VMEM((n_ctx * live, features), f32),
+            pltpu.VMEM((slots, features), f32),
             pltpu.VMEM((n_ctx, live, features), bf16),
             pltpu.VMEM((n_ctx, live, features), bf16),
             pltpu.VMEM((n_ctx, slots, features), f32),
-            pltpu.VMEM((n_ctx, slots, 128), f32),
-            pltpu.VMEM((n_ctx, slots, 128), f32),
+            pltpu.VMEM((n_ctx, live, 128), f32),
+            pltpu.VMEM((n_ctx, live, 128), f32),
             pltpu.VMEM((n_ctx, slots, 128), f32),
             pltpu.VMEM((n_ep, dense, HEAD_WIDTH), bf16),
             pltpu.VMEM((n, dense, HEAD_WIDTH), bf16),
@@ -644,26 +667,21 @@
             pltpu.VMEM((n, dense, HEAD_WIDTH), bf16),
             pltpu.VMEM((slots, features), f32),
             dma((3,)),
-            dma((kv_heads, 2)),
-            dma((3,)),
-            dma((n_ctx, kv_heads)),
-            dma((n_ctx, kv_heads)),
-            dma((n,)),
-            dma((n,)),
-            dma((chunks,)),
-            dma((chunks,)),
+            dma,
             dma((2,)),
-            dma((chunks,)),
-            dma((chunks,)),
+            dma,
+            dma((n_ctx - 1, kv_heads)),
+            dma,
             dma((2,)),
-            dma((n,)),
-            dma((n,)),
+            dma,
+            dma((2,)),
+            dma,
+            dma((2,)),
+            dma,
+            dma,
+            dma,
             dma((n_ctx,)),
-            dma((n_ctx,)),
-            dma((n_ctx,)),
-            dma((n_ctx,)),
-            dma((n_ctx,)),
-            dma((n_ctx,)),
+            *[dma] * 4,
         ],
         compiler_params=pltpu.CompilerParams(
             collective_id=0, has_side_effects=True, vmem_limit_bytes=60 * 1024 * 1024

time: 29.6 us -> 27.9 us (0.943)
  the two profiles are of different devices: /device:TPU:24 before, /device:TPU:8 now
where the time goes in v3:
time: 27.9 us; the launch traced here: 27.7 us
  Pallas kernels  26.9 us (96%)
  local copies, waits for them, and re-layouts  0.84 us (3%)
    pallas_call x1, Pallas kernels, shards(): pl.pallas_call(functools.partial(kernel, n_ctx, n_ep, n_tp), out_shape=pl...  26.9 us
    unnamed x1, local copies, waits for them, and re-layouts  0.84 us

profile of v3, /device:TPU:8, one launch (start us, length us, event | category | flops | bytes accessed | tf_op | source)
XLA Modules:
  0.0 27.7 jit_solution(712973338296326972)
XLA Ops:
  0.0 26.9 %shard_map.82 = bf16[1,128,2560]{2,1,0:T(8,128)(2,1)S(1)} custom-call(s32[1,128]{1,0:T(1,128)} %bitcast.3, bf16[1,2560]{1,0:T(2,128)(2,1)} %bitcast.2, bf16[1,128,2560]{2,1,0:T(8,128)(2,1)} %q_hbm.1, bf16[1,128,512]{2,1,0:T(8,128)(2,1)} %k_hbm.1, bf16[1,128,512]{2,1,0:T(8,128)(2,1)} %v_hbm.1, bf16[1,2560,1024]{2,1,0:T(8,128)(2,1)} %wg_hbm.1, ...), custom_call_target="tpu_custom_call" | custom-call | tf_op jit(solution)/shard_map/pallas_call | solution.py:636
  26.9 0.8 %copy.10 = bf16[1,128,2560]{2,1,0:T(8,128)(2,1)} copy(bf16[1,128,2560]{2,1,0:T(8,128)(2,1)S(1)} %shard_map.82) | data formatting | bytes 1310720

commit v4 on v3

--- a/solution.py
+++ b/solution.py
@@ -38,7 +38,7 @@
     ids_hbm, router_hbm, q_hbm, k_hbm, v_hbm, wg_hbm, wu_hbm, wd_hbm,
     out_ref,
     ids_ref, router_ref, q_ref, wgu, wd, kv, acc, row_max, totals, att,
-    q_own, q_out, q_in, q_pad, part_out, part_got, part_all, lse_out, lse_in, lse_all,
+    q_own, q_out, q_in, q_all, part_out, part_got, part_all, lse_out, lse_in, lse_all,
     out_rows, in_rows,
     members_a, part_a, part_in_a, hidden_a,
     members_b, part_b, part_in_b, hidden_b,
@@ -129,15 +129,12 @@
                 kv_copy(ctx, head).start()
 
     def relay(block, heads):
-        @pl.when(block >= 0)
+        @pl.when((block >= 0) & (ctx < last))
         def _():
             for head in heads:
                 copy = kv_copy(block, head)
                 copy.wait_recv()
-
-                @pl.when(ctx < last)
-                def _():
-                    copy.start()
+                copy.start()
 
     def q_copy(source, target):
         return pltpu.make_async_remote_copy(
@@ -301,7 +298,7 @@
         in_rows[me] = out_rows[ep]
 
     part_all[...] = jnp.zeros_like(part_all)
-    q_pad[...] = jnp.zeros_like(q_pad)
+    q_all[...] = jnp.zeros_like(q_all)
 
     @pl.when(ctx == 0)
     def _():
@@ -321,13 +318,14 @@
     def _():
         with scope("e_rows0"):
             send_rows()
-            push_own(range(2))
+            push_own(range(1))
 
     @pl.when(ctx > 0)
     def _():
         with scope("f_own"):
             own_landed()
-            push_own(range(kv_heads - 1))
+            push_own(range(2))
+            pl.when(ctx > 1)(lambda: push_own([2]))
             own_part()
 
     query_offset = lax.broadcasted_iota(jnp.int32, (rows, rows), 0)
@@ -369,43 +367,49 @@
         totals[head] = totals[head] * factor + jnp.sum(weights, axis=1, keepdims=True)
         acc[head] = acc[head] * factor + mix(weights, block, head)
 
-    def process_block(step):
-        @pl.when(ctx >= step)
-        def _():
-            for head in range(kv_heads):
-                process(ctx - step, head)
+    def visit(step):
+        def arrived(heads):
+            for head in heads:
+                kv_copy(ctx - step, head).wait_recv()
+
+        pl.when(ctx == last)(lambda: arrived(range(kv_heads)))
+        for head in range(kv_heads):
+            process(ctx - step, head)
+
+    def visit_by_head(step):
+        for head in range(kv_heads):
+            pl.when(ctx == last)(lambda: kv_copy(ctx - step, head).wait_recv())
+            relay(ctx - step, [head])
+            process(ctx - step, head)
 
     @pl.when(ctx < last)
     def _():
-        def answer(step, carry):
-            other = ctx + step
-
-            @pl.when(other <= last)
-            def _():
-                with scope("h_qwait"):
-                    q_copy(other, other).wait_recv()
-                with scope("i_qpart"):
-                    q_pad[:live] = q_in[other].astype(jnp.float32)
-                    mixed, lse = attend(q_pad, slots, None)
-                    lse_out[other] = lse[:live]
-                    for place in range(places):
-                        first = place % group * slots
-                        part_out[other, :, lanes(place)] = mixed[place // group][
-                            first:first + live
-                        ].astype(jnp.bfloat16)
-                    for copy in back_copies(ctx, other):
-                        copy.start()
-
-            return carry
-
-        lax.fori_loop(1, n_ctx, answer, 0)
-        pl.when(ctx == 0)(lambda: push_own(range(2, kv_heads)))
-        pl.when(ctx > 0)(lambda: push_own([kv_heads - 1]))
-
-    with scope("k_relay"):
-        pl.when(ctx > 1)(lambda: relay(ctx - 1, [0]))
-
-    def gate(indices, wide_ref, part, part_in, sent, got):
+        with scope("h_qwait"):
+            upper(lambda other: q_copy(other, other).wait_recv())
+        with scope("i_qpart"):
+            for other in range(n_ctx):
+                @pl.when(other > ctx)
+                def _():
+                    q_all[other * live:(other + 1) * live, :] = q_in[other].astype(jnp.float32)
+
+            tall = n_ctx * live
+            mixed, lse = attend(q_all, tall, None)
+            for other in range(n_ctx):
+                lse_out[other] = lse[other * live:(other + 1) * live]
+                for place in range(places):
+                    first = place % group * tall + other * live
+                    part_out[other, :, lanes(place)] = mixed[place // group][
+                        first:first + live
+                    ].astype(jnp.bfloat16)
+
+        with scope("j_give"):
+            def give_back(other):
+                for copy in back_copies(ctx, other):
+                    copy.start()
+
+            upper(give_back)
+            pl.when(ctx == 0)(lambda: push_own(range(1, kv_heads)))
+    def gate(indices, wide_ref, part, part_in, sent, got, between):
         for at, index in enumerate(indices):
             dense = in_rows[index].astype(jnp.float32)
             for place in range(places):
@@ -432,6 +436,7 @@
                 send_sem=sent, recv_sem=got.at[which],
                 device_id=peer, device_id_type=MESH,
             ).start()
+            between(chunk, chunks - 1)
 
     def activate(part, part_in, sent, got, hidden):
         chunks = part.shape[0]
@@ -482,11 +487,21 @@
         @pl.when(ctx > 0)
         def _():
             settled(in_rows.at[pl.ds(0, n_ep)], row_recv.at[0]).wait_recv()
+    def between_a(chunk, count):
+        if chunk == count // 2:
+            pl.when(ctx == 1)(lambda: push_own(range(2, kv_heads)))
+            pl.when(ctx > 1)(lambda: push_own([kv_heads - 1]))
+            pl.when(ctx > 1)(lambda: relay(ctx - 1, [0]))
+        if chunk == count:
+            pl.when(ctx == 1)(lambda: relay(ctx - 1, [0]))
+            pl.when(ctx > 1)(lambda: relay(ctx - 1, [1]))
+
+    def between_b(chunk, count):
+        if chunk == count // 2:
+            relay(ctx - 2, [1])
+
     with scope("m_gate_a"):
-        gate(first, members_a, *exchange_a)
-    with scope("n_relay"):
-        pl.when(ctx == 1)(lambda: relay(ctx - 1, [0]))
-        pl.when(ctx > 1)(lambda: relay(ctx - 1, range(1, kv_heads - 1)))
+        gate(first, members_a, *exchange_a, between_a)
 
     @pl.when(ctx > 0)
     def _():
@@ -516,19 +531,19 @@
         with scope("q_rows"):
             send_rows()
 
-    with scope("r_relay"):
-        pl.when(ctx == 1)(lambda: relay(ctx - 1, range(1, kv_heads)))
-        pl.when(ctx > 1)(lambda: relay(ctx - 1, [kv_heads - 1]))
-    with scope("s_down_a"):
+    with scope("r_down_a"):
         w_copies[2].wait()
         activate(*exchange_a, hidden_a)
         down(first, hidden_a)
         first_owners(lambda other: down_copy(other, me).start())
         pl.when(ctx == 0)(keep_own)
+    with scope("s_relay"):
+        pl.when(ctx == 1)(lambda: relay(ctx - 1, range(1, kv_heads)))
+        pl.when(ctx > 1)(lambda: relay(ctx - 1, range(2, kv_heads)))
     with scope("t_block1"):
-        process_block(1)
+        pl.when(ctx > 1)(lambda: visit(1))
     with scope("u_relay"):
-        relay(ctx - 2, range(2))
+        relay(ctx - 2, [0])
     with scope("v_rows_b"):
         @pl.when(ctx == 0)
         def _():
@@ -539,28 +554,31 @@
             settled(in_rows.at[pl.ds(0, n - n_ep - 1)], row_recv.at[1]).wait_recv()
 
     with scope("w_gate_b"):
-        gate(later, members_b, *exchange_b)
+        gate(later, members_b, *exchange_b, between_b)
     with scope("x_relay"):
-        relay(ctx - 2, range(2, kv_heads))
+        relay(ctx - 2, range(2, kv_heads - 1))
+    early = (tp == n_tp - 1) & (ctx > 2)
     with scope("xa_block2"):
-        process_block(2)
+        pl.when(early)(lambda: visit(2))
     with scope("xb_down_b"):
         activate(*exchange_b, hidden_b)
         down(later, hidden_b)
         later_owners(lambda other: down_copy(other, me).start())
         pl.when(ctx > 0)(keep_own)
 
-    def visit(step, carry):
-        @pl.when(ctx >= step)
+    def remaining(step, carry):
+        pl.when(ctx >= step)(lambda: visit_by_head(step))
+        return carry
+
+    with scope("xc_visit"):
+        relay(ctx - 2, [kv_heads - 1])
+        left = jnp.where(ctx == 1, 1, 2)
+
+        @pl.when((ctx > 0) & jnp.logical_not(early))
         def _():
-            for head in range(kv_heads):
-                relay(ctx - step, [head])
-                process(ctx - step, head)
-
-        return carry
-
-    with scope("xc_visit"):
-        lax.fori_loop(3, n_ctx, visit, 0)
+            visit(left)
+
+        lax.fori_loop(3, n_ctx, remaining, 0)
 
     with scope("xd_norm"):
         for head in range(kv_heads):
@@ -652,7 +670,7 @@
             pltpu.VMEM((slots, features), f32),
             pltpu.VMEM((live, features), bf16),
             pltpu.VMEM((n_ctx, live, features), bf16),
-            pltpu.VMEM((slots, features), f32),
+            pltpu.VMEM((n_ctx * live, features), f32),
             pltpu.VMEM((n_ctx, live, features), bf16),
             pltpu.VMEM((n_ctx, live, features), bf16),
             pltpu.VMEM((n_ctx, slots, features), f32),

time: 27.9 us -> 26.7 us (0.957)
  the two profiles are of different devices: /device:TPU:8 before, /device:TPU:24 now
where the time goes in v4:
time: 26.7 us; the launch traced here: 26.5 us
  Pallas kernels  25.7 us (96%)
  local copies, waits for them, and re-layouts  0.84 us (3%)
    pallas_call x1, Pallas kernels, shards(): pl.pallas_call(functools.partial(kernel, n_ctx, n_ep, n_tp), out_shape=pl...  25.7 us
    unnamed x1, local copies, waits for them, and re-layouts  0.84 us

profile of v4, /device:TPU:24, one launch (start us, length us, event | category | flops | bytes accessed | tf_op | source)
XLA Modules:
  0.0 26.5 jit_solution(5547627477550132314)
XLA Ops:
  0.0 25.7 %shard_map.82 = bf16[1,128,2560]{2,1,0:T(8,128)(2,1)S(1)} custom-call(s32[1,128]{1,0:T(1,128)} %bitcast.3, bf16[1,2560]{1,0:T(2,128)(2,1)} %bitcast.2, bf16[1,128,2560]{2,1,0:T(8,128)(2,1)} %q_hbm.1, bf16[1,128,512]{2,1,0:T(8,128)(2,1)} %k_hbm.1, bf16[1,128,512]{2,1,0:T(8,128)(2,1)} %v_hbm.1, bf16[1,2560,1024]{2,1,0:T(8,128)(2,1)} %wg_hbm.1, ...), custom_call_target="tpu_custom_call" | custom-call | tf_op jit(solution)/shard_map/pallas_call | solution.py:654
  25.7 0.8 %copy.10 = bf16[1,128,2560]{2,1,0:T(8,128)(2,1)} copy(bf16[1,128,2560]{2,1,0:T(8,128)(2,1)S(1)} %shard_map.82) | data formatting | bytes 1310720

commit v5 on v4

--- a/solution.py
+++ b/solution.py
@@ -497,8 +497,7 @@
             pl.when(ctx > 1)(lambda: relay(ctx - 1, [1]))
 
     def between_b(chunk, count):
-        if chunk == count // 2:
-            relay(ctx - 2, [1])
+        pass
 
     with scope("m_gate_a"):
         gate(first, members_a, *exchange_a, between_a)
@@ -556,7 +555,7 @@
     with scope("w_gate_b"):
         gate(later, members_b, *exchange_b, between_b)
     with scope("x_relay"):
-        relay(ctx - 2, range(2, kv_heads - 1))
+        relay(ctx - 2, [1])
     early = (tp == n_tp - 1) & (ctx > 2)
     with scope("xa_block2"):
         pl.when(early)(lambda: visit(2))
@@ -570,41 +569,14 @@
         pl.when(ctx >= step)(lambda: visit_by_head(step))
         return carry
 
-    with scope("xc_visit"):
-        relay(ctx - 2, [kv_heads - 1])
-        left = jnp.where(ctx == 1, 1, 2)
-
-        @pl.when((ctx > 0) & jnp.logical_not(early))
-        def _():
-            visit(left)
-
-        lax.fori_loop(3, n_ctx, remaining, 0)
-
-    with scope("xd_norm"):
-        for head in range(kv_heads):
-            normed = (acc[head] / totals[head]).astype(jnp.bfloat16)
-            for j in range(group):
-                att[:, lanes(head * group + j)] = normed[j * rows:(j + 1) * rows]
+    def norm(head):
+        normed = (acc[head] / totals[head]).astype(jnp.bfloat16)
+        for j in range(group):
+            att[:, lanes(head * group + j)] = normed[j * rows:(j + 1) * rows]
+
+    def settle_down():
+        settled(down_in.at[pl.ds(0, n - 1)], down_recv).wait_recv()
         returned[...] = jnp.zeros_like(returned)
-
-    with scope("xe_sent"):
-        settled(in_rows.at[pl.ds(0, n - 1)], row_send).wait_send()
-        settled(part_a, a_send).wait_send()
-        settled(part_b, b_send).wait_send()
-
-        def drain(index):
-            if index:
-                settled(q_in.at[pl.ds(0, index)], q_send).wait_send()
-            if index < last:
-                settled(part_out.at[pl.ds(0, last - index)], back_send).wait_send()
-                settled(lse_out.at[pl.ds(0, last - index)], lse_send).wait_send()
-                settled(kv.at[pl.ds(0, index + 1)], kv_send).wait_send()
-
-        by_ctx(drain)
-
-    with scope("xf_downwait"):
-        settled(down_in.at[pl.ds(0, n - 1)], down_recv).wait_recv()
-    with scope("xg_final"):
         for expert in range(n_ep):
             total = down_in[expert * n_ctx].astype(jnp.float32)
             for index in range(1, n_ctx):
@@ -614,15 +586,72 @@
                 returned[expert * CAP:(expert + 1) * CAP, lanes(place)] = total[
                     place * CAP:(place + 1) * CAP
                 ]
-        for start, size in tiles_of(features, 512):
-            routed = lax.dot_general(
-                spread, returned[:, start:start + size].astype(jnp.bfloat16),
-                (((0,), (0,)), ((), ())), preferred_element_type=jnp.float32,
-            )
-            out_ref[0, :, start:start + size] = (
-                att[:, start:start + size].astype(jnp.float32) + routed
-            ).astype(jnp.bfloat16)
+
+    def finish(head):
+        width = group * HEAD_WIDTH
+        span = slice(head * width, (head + 1) * width)
+        routed = lax.dot_general(
+            spread, returned[:, span].astype(jnp.bfloat16),
+            (((0,), (0,)), ((), ())), preferred_element_type=jnp.float32,
+        )
+        out_ref[0, :, span] = (att[:, span].astype(jnp.float32) + routed).astype(jnp.bfloat16)
+
+    with scope("xc_visit"):
+        relay(ctx - 2, range(2, kv_heads))
+        left = jnp.where(ctx == 1, 1, 2)
+
+        @pl.when((ctx > 0) & jnp.logical_not(early))
+        def _():
+            visit(left)
+
+    ends = (ctx == last) & (last > 2)
+
+    @pl.when(ends)
+    def _():
+        with scope("xd_visit"):
+            lax.fori_loop(3, last, remaining, 0)
+
+            def arrived(head):
+                kv_copy(0, head).wait_recv()
+                process(0, head)
+                norm(head)
+
+            for head in range(kv_heads - 1):
+                arrived(head)
+        with scope("xe_down"):
+            settle_down()
+            for head in range(kv_heads - 1):
+                finish(head)
+        with scope("xf_last"):
+            arrived(kv_heads - 1)
+            finish(kv_heads - 1)
+
+    @pl.when(jnp.logical_not(ends))
+    def _():
+        lax.fori_loop(3, n_ctx, remaining, 0)
+        with scope("xd_norm"):
+            for head in range(kv_heads):
+                norm(head)
+        with scope("xe_down"):
+            settle_down()
+        with scope("xg_final"):
+            for head in range(kv_heads):
+                finish(head)
+
     with scope("xh_sent"):
+        settled(in_rows.at[pl.ds(0, n - 1)], row_send).wait_send()
+        settled(part_a, a_send).wait_send()
+        settled(part_b, b_send).wait_send()
+
+        def drain(index):
+            if index:
+                settled(q_in.at[pl.ds(0, index)], q_send).wait_send()
+            if index < last:
+                settled(part_out.at[pl.ds(0, last - index)], back_send).wait_send()
+                settled(lse_out.at[pl.ds(0, last - index)], lse_send).wait_send()
+                settled(kv.at[pl.ds(0, index + 1)], kv_send).wait_send()
+
+        by_ctx(drain)
         settled(down_out.at[pl.ds(0, n - 1)], down_send).wait_send()
 
 

time: 26.7 us -> 26.4 us (0.989); the launches traced: 26.5 us -> 25.9 us
  Pallas kernels: 25.7 us -> 25 us
    pallas_call x1, Pallas kernels: 25.7 us -> 25 us  [shards(): pl.pallas_call(functools.partial(kernel, n_ctx, n_ep, n_tp), out_shape=pl...]
where the time goes in v5:
time: 26.4 us; the launch traced here: 25.9 us
  Pallas kernels  25 us (95%)
  local copies, waits for them, and re-layouts  0.84 us (3%)
    pallas_call x1, Pallas kernels, shards(): pl.pallas_call(functools.partial(kernel, n_ctx, n_ep, n_tp), out_shape=pl...  25 us
    unnamed x1, local copies, waits for them, and re-layouts  0.84 us

profile of v5, /device:TPU:24, one launch (start us, length us, event | category | flops | bytes accessed | tf_op | source)
XLA Modules:
  0.0 25.9 jit_solution(16067629903409280053)
XLA Ops:
  0.0 25.0 %shard_map.82 = bf16[1,128,2560]{2,1,0:T(8,128)(2,1)S(1)} custom-call(s32[1,128]{1,0:T(1,128)} %bitcast.3, bf16[1,2560]{1,0:T(2,128)(2,1)} %bitcast.2, bf16[1,128,2560]{2,1,0:T(8,128)(2,1)} %q_hbm.1, bf16[1,128,512]{2,1,0:T(8,128)(2,1)} %k_hbm.1, bf16[1,128,512]{2,1,0:T(8,128)(2,1)} %v_hbm.1, bf16[1,2560,1024]{2,1,0:T(8,128)(2,1)} %wg_hbm.1, ...), custom_call_target="tpu_custom_call" | custom-call | tf_op jit(solution)/shard_map/pallas_call | solution.py:683
  25.1 0.8 %copy.10 = bf16[1,128,2560]{2,1,0:T(8,128)(2,1)} copy(bf16[1,128,2560]{2,1,0:T(8,128)(2,1)S(1)} %shard_map.82) | data formatting | bytes 1310720

commit v6 on v5

--- a/solution.py
+++ b/solution.py
@@ -53,6 +53,7 @@
     n = n_ctx * n_ep
     me = ep * n_ctx + ctx
     last = n_ctx - 1
+    home = last - 1
     rows, features = q_ref.shape
     kv_heads = kv.shape[1]
     places = features // HEAD_WIDTH
@@ -115,26 +116,38 @@
         for index in range(n_ctx):
             pl.when(ctx == index)(functools.partial(body, index))
 
-    def kv_copy(block, head):
-        return pltpu.make_async_remote_copy(
-            src_ref=kv.at[block, head], dst_ref=kv.at[block, head],
-            send_sem=kv_send, recv_sem=kv_recv.at[block, head],
-            device_id={"ctx": ctx + 1}, device_id_type=MESH,
-        )
+    def kv_copies(block, head):
+        parts = [kv.at[block, head]]
+        if head == kv_heads - 1:
+            parts = [kv.at[block, head, 0], kv.at[block, head, 1]]
+        return [
+            pltpu.make_async_remote_copy(
+                src_ref=part, dst_ref=part,
+                send_sem=kv_send, recv_sem=kv_recv.at[block, head + index],
+                device_id={"ctx": ctx + 1}, device_id_type=MESH,
+            )
+            for index, part in enumerate(parts)
+        ]
 
     def push_own(heads):
         @pl.when(ctx < last)
         def _():
             for head in heads:
-                kv_copy(ctx, head).start()
+                for copy in kv_copies(ctx, head):
+                    copy.start()
 
     def relay(block, heads):
         @pl.when((block >= 0) & (ctx < last))
         def _():
             for head in heads:
-                copy = kv_copy(block, head)
+                for copy in kv_copies(block, head):
+                    copy.wait_recv()
+                    copy.start()
+
+    def arrive(block, heads):
+        for head in heads:
+            for copy in kv_copies(block, head):
                 copy.wait_recv()
-                copy.start()
 
     def q_copy(source, target):
         return pltpu.make_async_remote_copy(
@@ -143,12 +156,13 @@
             device_id={"ctx": target}, device_id_type=MESH,
         )
 
-    def back_copies(source, target):
+    def back_copies(target):
+        slot = jnp.where(target == last, n_ctx, 0) + ctx
         return [
             pltpu.make_async_remote_copy(
-                src_ref=out.at[target], dst_ref=into.at[source],
+                src_ref=out.at[target], dst_ref=into.at[slot],
                 send_sem=sent, recv_sem=got,
-                device_id={"ctx": target}, device_id_type=MESH,
+                device_id={"ctx": jnp.minimum(target, home)}, device_id_type=MESH,
             )
             for out, into, sent, got in (
                 (part_out, part_got, back_send, back_recv),
@@ -163,9 +177,11 @@
             device_id={"ep": other // n_ctx, "ctx": other % n_ctx}, device_id_type=MESH,
         )
 
-    def row_copy(other, source):
+    def row_copy(other, which):
         got = row_recv.at[jnp.where(ctx == 0, 0, 1)]
-        return to_index(other, out_rows.at[other // n_ctx], in_rows, row_send, got, source)
+        return to_index(
+            other, out_rows.at[which, other // n_ctx], in_rows, row_send.at[which], got, me + which
+        )
 
     def down_copy(other, source):
         return to_index(other, down_out.at[other], down_in, down_send, down_recv, source)
@@ -280,22 +296,24 @@
         seen = key_lane <= jnp.concatenate([row_place] * group, axis=0)
         mixed, lse = attend(q_own, slots, seen)
         lse_all[...] = jnp.full_like(lse_all, MASKED)
-        lse_all[ctx] = lse
+        lse_all[0, ctx] = lse
         for head in range(kv_heads):
             for j in range(group):
-                part_all[ctx, :, lanes(head * group + j)] = mixed[head][
+                part_all[0, ctx, :, lanes(head * group + j)] = mixed[head][
                     j * slots:(j + 1) * slots
                 ]
 
-    def put_row(place, picked):
+        return mixed, lse
+
+    def put_row(which, place, picked):
         for expert in range(n_ep):
-            out_rows[expert, place * CAP:(place + 1) * CAP] = picked[
+            out_rows[which, expert, place * CAP:(place + 1) * CAP] = picked[
                 expert * CAP:(expert + 1) * CAP
             ].astype(jnp.bfloat16)
 
-    def send_rows():
-        others(lambda other: row_copy(other, me).start())
-        in_rows[me] = out_rows[ep]
+    def send_rows(which):
+        others(lambda other: row_copy(other, which).start())
+        in_rows[me + which] = out_rows[which, ep]
 
     part_all[...] = jnp.zeros_like(part_all)
     q_all[...] = jnp.zeros_like(q_all)
@@ -306,7 +324,7 @@
             own_landed()
             own_part()
             for place in range(places):
-                put_row(place, part_all[0, :, lanes(place)])
+                put_row(0, place, part_all[0, 0, :, lanes(place)])
 
     with scope("c_barrier"):
         pl.semaphore_wait(barrier, n - 1 + n_tp - 1)
@@ -317,7 +335,7 @@
     @pl.when(ctx == 0)
     def _():
         with scope("e_rows0"):
-            send_rows()
+            send_rows(0)
             push_own(range(1))
 
     @pl.when(ctx > 0)
@@ -325,8 +343,19 @@
         with scope("f_own"):
             own_landed()
             push_own(range(2))
-            pl.when(ctx > 1)(lambda: push_own([2]))
-            own_part()
+            pl.when(ctx > 1)(lambda: push_own(range(2, kv_heads)))
+            mixed, lse = own_part()
+
+            @pl.when(ctx == last)
+            def _():
+                lse_out[last] = lse[:live]
+                for place in range(places):
+                    first = place % group * slots
+                    part_out[last, :, lanes(place)] = mixed[place // group][
+                        first:first + live
+                    ].astype(jnp.bfloat16)
+                for copy in back_copies(last):
+                    copy.start()
 
     query_offset = lax.broadcasted_iota(jnp.int32, (rows, rows), 0)
     key_offset = lax.broadcasted_iota(jnp.int32, (rows, rows), 1)
@@ -357,7 +386,7 @@
             )
             acc[head] = mix(weights, ctx, head)
 
-    def process(block, head):
+    def process(block, head, before_values=None):
         raw = scores(block, head)
         old_max = row_max[head]
         new_max = jnp.maximum(old_max, jnp.max(raw, axis=1, keepdims=True))
@@ -365,20 +394,18 @@
         weights = jnp.exp2((raw - new_max) * EXP2_SCALE)
         row_max[head] = new_max
         totals[head] = totals[head] * factor + jnp.sum(weights, axis=1, keepdims=True)
+        if before_values is not None:
+            before_values()
         acc[head] = acc[head] * factor + mix(weights, block, head)
 
     def visit(step):
-        def arrived(heads):
-            for head in heads:
-                kv_copy(ctx - step, head).wait_recv()
-
-        pl.when(ctx == last)(lambda: arrived(range(kv_heads)))
+        pl.when(ctx == last)(lambda: arrive(ctx - step, range(kv_heads)))
         for head in range(kv_heads):
             process(ctx - step, head)
 
     def visit_by_head(step):
         for head in range(kv_heads):
-            pl.when(ctx == last)(lambda: kv_copy(ctx - step, head).wait_recv())
+            pl.when(ctx == last)(lambda: arrive(ctx - step, [head]))
             relay(ctx - step, [head])
             process(ctx - step, head)
 
@@ -394,6 +421,15 @@
 
             tall = n_ctx * live
             mixed, lse = attend(q_all, tall, None)
+            @pl.when(ctx == home)
+            def _():
+                lse_all[1, home, :live] = lse[last * live:]
+                for place in range(places):
+                    first = place % group * tall + last * live
+                    part_all[1, home, :live, lanes(place)] = mixed[place // group][
+                        first:first + live
+                    ]
+
             for other in range(n_ctx):
                 lse_out[other] = lse[other * live:(other + 1) * live]
                 for place in range(places):
@@ -404,10 +440,10 @@
 
         with scope("j_give"):
             def give_back(other):
-                for copy in back_copies(ctx, other):
+                for copy in back_copies(other):
                     copy.start()
 
-            upper(give_back)
+            pl.when(ctx < home)(lambda: upper(give_back))
             pl.when(ctx == 0)(lambda: push_own(range(1, kv_heads)))
     def gate(indices, wide_ref, part, part_in, sent, got, between):
         for at, index in enumerate(indices):
@@ -488,47 +524,60 @@
         def _():
             settled(in_rows.at[pl.ds(0, n_ep)], row_recv.at[0]).wait_recv()
     def between_a(chunk, count):
-        if chunk == count // 2:
+        if chunk == (count + 1) // 2:
             pl.when(ctx == 1)(lambda: push_own(range(2, kv_heads)))
-            pl.when(ctx > 1)(lambda: push_own([kv_heads - 1]))
             pl.when(ctx > 1)(lambda: relay(ctx - 1, [0]))
-        if chunk == count:
-            pl.when(ctx == 1)(lambda: relay(ctx - 1, [0]))
-            pl.when(ctx > 1)(lambda: relay(ctx - 1, [1]))
 
     def between_b(chunk, count):
-        pass
+        if chunk == (count + 1) // 2:
+            relay(ctx - 2, [0])
 
     with scope("m_gate_a"):
         gate(first, members_a, *exchange_a, between_a)
 
-    @pl.when(ctx > 0)
+    def combine(which):
+        peak = jnp.max(lse_all[which], axis=0)
+        shares = [jnp.exp2(lse_all[which, other] - peak) for other in range(n_ctx)]
+        share_total = functools.reduce(jnp.add, shares)
+        shares = [share / share_total for share in shares]
+        for place in range(places):
+            put_row(which, place, functools.reduce(jnp.add, [
+                shares[other][:, place:place + 1] * part_all[which, other, :, lanes(place)]
+                for other in range(n_ctx)
+            ]))
+
+    def take(which, other):
+        slot = which * n_ctx + other
+        part_all[which, other, :live] = part_got[slot].astype(jnp.float32)
+        lse_all[which, other, :live] = lse_in[slot]
+
+    @pl.when((ctx > 0) & (ctx < last))
     def _():
         with scope("o_takeback"):
             def take_back(count):
-                if count:
+                if 0 < count < last:
+                    count = 2 * count + 1 if count == home else count
                     settled(part_got.at[pl.ds(0, count)], back_recv).wait_recv()
                     settled(lse_in.at[pl.ds(0, count)], lse_recv).wait_recv()
 
             by_ctx(take_back)
         with scope("p_combine"):
-            for other in range(last):
-                @pl.when(other < ctx)
-                def _():
-                    part_all[other, :live] = part_got[other].astype(jnp.float32)
-                    lse_all[other, :live] = lse_in[other]
-
-            peak = jnp.max(lse_all[...], axis=0)
-            shares = [jnp.exp2(lse_all[other] - peak) for other in range(n_ctx)]
-            share_total = functools.reduce(jnp.add, shares)
-            shares = [share / share_total for share in shares]
-            for place in range(places):
-                put_row(place, functools.reduce(jnp.add, [
-                    shares[other][:, place:place + 1] * part_all[other, :, lanes(place)]
-                    for other in range(n_ctx)
-                ]))
+            for other in range(home):
+                pl.when(other < ctx)(functools.partial(take, 0, other))
+
+            @pl.when(ctx == home)
+            def _():
+                for other in range(n_ctx):
+                    if other != home:
+                        take(1, other)
+                combine(1)
+                send_rows(1)
+
+            combine(0)
         with scope("q_rows"):
-            send_rows()
+            send_rows(0)
+            pl.when(ctx == 1)(lambda: relay(ctx - 1, [0]))
+            pl.when(ctx > 1)(lambda: relay(ctx - 1, [1]))
 
     with scope("r_down_a"):
         w_copies[2].wait()
@@ -541,22 +590,26 @@
         pl.when(ctx > 1)(lambda: relay(ctx - 1, range(2, kv_heads)))
     with scope("t_block1"):
         pl.when(ctx > 1)(lambda: visit(1))
-    with scope("u_relay"):
-        relay(ctx - 2, [0])
     with scope("v_rows_b"):
-        @pl.when(ctx == 0)
+        @pl.when((ctx == 0) | (ctx == last))
         def _():
             settled(in_rows.at[pl.ds(0, n - n_ep)], row_recv.at[1]).wait_recv()
 
-        @pl.when(ctx > 0)
+        @pl.when((ctx > 0) & (ctx < home))
         def _():
             settled(in_rows.at[pl.ds(0, n - n_ep - 1)], row_recv.at[1]).wait_recv()
 
+        @pl.when(ctx == home)
+        def _():
+            settled(in_rows.at[pl.ds(0, n - n_ep - 2)], row_recv.at[1]).wait_recv()
+
     with scope("w_gate_b"):
         gate(later, members_b, *exchange_b, between_b)
+    ahead = tp == n_tp - 1
+    early = ahead & (ctx > 2)
     with scope("x_relay"):
         relay(ctx - 2, [1])
-    early = (tp == n_tp - 1) & (ctx > 2)
+        pl.when(ahead)(lambda: relay(ctx - 2, range(2, kv_heads)))
     with scope("xa_block2"):
         pl.when(early)(lambda: visit(2))
     with scope("xb_down_b"):
@@ -597,7 +650,7 @@
         out_ref[0, :, span] = (att[:, span].astype(jnp.float32) + routed).astype(jnp.bfloat16)
 
     with scope("xc_visit"):
-        relay(ctx - 2, range(2, kv_heads))
+        pl.when(jnp.logical_not(ahead))(lambda: relay(ctx - 2, range(2, kv_heads)))
         left = jnp.where(ctx == 1, 1, 2)
 
         @pl.when((ctx > 0) & jnp.logical_not(early))
@@ -612,8 +665,9 @@
             lax.fori_loop(3, last, remaining, 0)
 
             def arrived(head):
-                kv_copy(0, head).wait_recv()
-                process(0, head)
+                first, *rest = kv_copies(0, head)
+                first.wait_recv()
+                process(0, head, rest[0].wait_recv if rest else None)
                 norm(head)
 
             for head in range(kv_heads - 1):
@@ -639,16 +693,19 @@
                 finish(head)
 
     with scope("xh_sent"):
-        settled(in_rows.at[pl.ds(0, n - 1)], row_send).wait_send()
         settled(part_a, a_send).wait_send()
         settled(part_b, b_send).wait_send()
 
         def drain(index):
             if index:
                 settled(q_in.at[pl.ds(0, index)], q_send).wait_send()
+            given = {home: 0, last: 1}.get(index, last - index)
+            if given:
+                settled(part_out.at[pl.ds(0, given)], back_send).wait_send()
+                settled(lse_out.at[pl.ds(0, given)], lse_send).wait_send()
+            for which in range({home: 2, last: 0}.get(index, 1)):
+                settled(in_rows.at[pl.ds(0, n - 1)], row_send.at[which]).wait_send()
             if index < last:
-                settled(part_out.at[pl.ds(0, last - index)], back_send).wait_send()
-                settled(lse_out.at[pl.ds(0, last - index)], lse_send).wait_send()
                 settled(kv.at[pl.ds(0, index + 1)], kv_send).wait_send()
 
         by_ctx(drain)
@@ -701,12 +758,12 @@
             pltpu.VMEM((n_ctx, live, features), bf16),
             pltpu.VMEM((n_ctx * live, features), f32),
             pltpu.VMEM((n_ctx, live, features), bf16),
-            pltpu.VMEM((n_ctx, live, features), bf16),
-            pltpu.VMEM((n_ctx, slots, features), f32),
+            pltpu.VMEM((2 * n_ctx, live, features), bf16),
+            pltpu.VMEM((2, n_ctx, slots, features), f32),
             pltpu.VMEM((n_ctx, live, 128), f32),
-            pltpu.VMEM((n_ctx, live, 128), f32),
-            pltpu.VMEM((n_ctx, slots, 128), f32),
-            pltpu.VMEM((n_ep, dense, HEAD_WIDTH), bf16),
+            pltpu.VMEM((2 * n_ctx, live, 128), f32),
+            pltpu.VMEM((2, n_ctx, slots, 128), f32),
+            pltpu.VMEM((2, n_ep, dense, HEAD_WIDTH), bf16),
             pltpu.VMEM((n, dense, HEAD_WIDTH), bf16),
             *batch(n_ep * CAP),
             *batch((n - n_ep) * CAP),
@@ -717,8 +774,8 @@
             dma,
             dma((2,)),
             dma,
-            dma((n_ctx - 1, kv_heads)),
-            dma,
+            dma((n_ctx - 1, kv_heads + 1)),
+            dma((2,)),
             dma((2,)),
             dma,
             dma((2,)),

time: 26.4 us -> 25.6 us (0.970); the launches traced: 25.9 us -> 25.4 us
  Pallas kernels: 25 us -> 24.6 us
    pallas_call x1, Pallas kernels: 25 us -> 24.6 us  [shards(): pl.pallas_call(functools.partial(kernel, n_ctx, n_ep, n_tp), out_shape=pl...]
where the time goes in v6:
time: 25.6 us; the launch traced here: 25.4 us
  Pallas kernels  24.6 us (96%)
  local copies, waits for them, and re-layouts  0.84 us (3%)
    pallas_call x1, Pallas kernels, shards(): pl.pallas_call(functools.partial(kernel, n_ctx, n_ep, n_tp), out_shape=pl...  24.6 us
    unnamed x1, local copies, waits for them, and re-layouts  0.84 us

profile of v6, /device:TPU:24, one launch (start us, length us, event | category | flops | bytes accessed | tf_op | source)
XLA Modules:
  0.0 25.4 jit_solution(1211311293993464061)
XLA Ops:
  0.0 24.6 %shard_map.82 = bf16[1,128,2560]{2,1,0:T(8,128)(2,1)S(1)} custom-call(s32[1,128]{1,0:T(1,128)} %bitcast.3, bf16[1,2560]{1,0:T(2,128)(2,1)} %bitcast.2, bf16[1,128,2560]{2,1,0:T(8,128)(2,1)} %q_hbm.1, bf16[1,128,512]{2,1,0:T(8,128)(2,1)} %k_hbm.1, bf16[1,128,512]{2,1,0:T(8,128)(2,1)} %v_hbm.1, bf16[1,2560,1024]{2,1,0:T(8,128)(2,1)} %wg_hbm.1, ...), custom_call_target="tpu_custom_call" | custom-call | tf_op jit(solution)/shard_map/pallas_call | solution.py:740
  24.6 0.8 %copy.10 = bf16[1,128,2560]{2,1,0:T(8,128)(2,1)} copy(bf16[1,128,2560]{2,1,0:T(8,128)(2,1)S(1)} %shard_map.82) | data formatting | bytes 1310720

commit v7 on v6

--- a/solution.py
+++ b/solution.py
@@ -670,15 +670,18 @@
                 process(0, head, rest[0].wait_recv if rest else None)
                 norm(head)
 
-            for head in range(kv_heads - 1):
-                arrived(head)
-        with scope("xe_down"):
-            settle_down()
-            for head in range(kv_heads - 1):
-                finish(head)
-        with scope("xf_last"):
-            arrived(kv_heads - 1)
-            finish(kv_heads - 1)
+            def run(before):
+                for head in range(before):
+                    arrived(head)
+                settle_down()
+                for head in range(before):
+                    finish(head)
+                for head in range(before, kv_heads):
+                    arrived(head)
+                    finish(head)
+
+            pl.when(ahead)(lambda: run(kv_heads))
+            pl.when(jnp.logical_not(ahead))(lambda: run(kv_heads - 2))
 
     @pl.when(jnp.logical_not(ends))
     def _():

time: 25.6 us -> 25.3 us (0.988)
  Pallas kernels: 24.6 us -> 24.3 us
    pallas_call x1, Pallas kernels: 24.6 us -> 24.3 us  [shards(): pl.pallas_call(functools.partial(kernel, n_ctx, n_ep, n_tp), out_shape=pl...]
where the time goes in v7:
time: 25.3 us; the launch traced here: 25.1 us
  Pallas kernels  24.3 us (96%)
  local copies, waits for them, and re-layouts  0.84 us (3%)
    pallas_call x1, Pallas kernels, shards(): pl.pallas_call(functools.partial(kernel, n_ctx, n_ep, n_tp), out_shape=pl...  24.3 us
    unnamed x1, local copies, waits for them, and re-layouts  0.84 us

profile of v7, /device:TPU:24, one launch (start us, length us, event | category | flops | bytes accessed | tf_op | source)
XLA Modules:
  0.0 25.1 jit_solution(6840495322512804737)
XLA Ops:
  0.0 24.3 %shard_map.82 = bf16[1,128,2560]{2,1,0:T(8,128)(2,1)S(1)} custom-call(s32[1,128]{1,0:T(1,128)} %bitcast.3, bf16[1,2560]{1,0:T(2,128)(2,1)} %bitcast.2, bf16[1,128,2560]{2,1,0:T(8,128)(2,1)} %q_hbm.1, bf16[1,128,512]{2,1,0:T(8,128)(2,1)} %k_hbm.1, bf16[1,128,512]{2,1,0:T(8,128)(2,1)} %v_hbm.1, bf16[1,2560,1024]{2,1,0:T(8,128)(2,1)} %wg_hbm.1, ...), custom_call_target="tpu_custom_call" | custom-call | tf_op jit(solution)/shard_map/pallas_call | solution.py:743
  24.3 0.8 %copy.10 = bf16[1,128,2560]{2,1,0:T(8,128)(2,1)} copy(bf16[1,128,2560]{2,1,0:T(8,128)(2,1)S(1)} %shard_map.82) | data formatting | bytes 1310720

commit v8 on v7

--- a/solution.py
+++ b/solution.py
@@ -676,8 +676,14 @@
                 settle_down()
                 for head in range(before):
                     finish(head)
-                for head in range(before, kv_heads):
-                    arrived(head)
+                final = list(range(before, kv_heads))
+                values = [copy for head in final for copy in kv_copies(0, head)]
+                for copy in values[:-1]:
+                    copy.wait_recv()
+                for head in final:
+                    process(0, head, values[-1].wait_recv if head == kv_heads - 1 else None)
+                for head in final:
+                    norm(head)
                     finish(head)
 
             pl.when(ahead)(lambda: run(kv_heads))

time: 25.3 us -> 25.4 us (level)
  no operation moved by 1% of the time
where the time goes in v8:
time: 25.4 us; the launch traced here: 25.2 us
  Pallas kernels  24.4 us (96%)
  local copies, waits for them, and re-layouts  0.84 us (3%)
    pallas_call x1, Pallas kernels, shards(): pl.pallas_call(functools.partial(kernel, n_ctx, n_ep, n_tp), out_shape=pl...  24.4 us
    unnamed x1, local copies, waits for them, and re-layouts  0.84 us

profile of v8, /device:TPU:24, one launch (start us, length us, event | category | flops | bytes accessed | tf_op | source)
XLA Modules:
  0.0 25.2 jit_solution(16783106550684548177)
XLA Ops:
  0.0 24.4 %shard_map.82 = bf16[1,128,2560]{2,1,0:T(8,128)(2,1)S(1)} custom-call(s32[1,128]{1,0:T(1,128)} %bitcast.3, bf16[1,2560]{1,0:T(2,128)(2,1)} %bitcast.2, bf16[1,128,2560]{2,1,0:T(8,128)(2,1)} %q_hbm.1, bf16[1,128,512]{2,1,0:T(8,128)(2,1)} %k_hbm.1, bf16[1,128,512]{2,1,0:T(8,128)(2,1)} %v_hbm.1, bf16[1,2560,1024]{2,1,0:T(8,128)(2,1)} %wg_hbm.1, ...), custom_call_target="tpu_custom_call" | custom-call | tf_op jit(solution)/shard_map/pallas_call | solution.py:749
  24.4 0.8 %copy.10 = bf16[1,128,2560]{2,1,0:T(8,128)(2,1)} copy(bf16[1,128,2560]{2,1,0:T(8,128)(2,1)S(1)} %shard_map.82) | data formatting | bytes 1310720
